TPU v7x, 32 devices: a 4x4x1 block of a 4x4x8 slice. The times are simulated.
32 devices in a mesh: dp: 1 (over z), ep: 32 (over y, x, core).
Axes of the slice: x: 4, y: 4, z: 1, core: 2. Of those that a mesh axis runs over, the one named last changes fastest.
The devices are a block of a 4x4x8 slice.
Arguments:
- tokens: bfloat16 [12288, 1024], P(('dp', 'ep'))
- expert_ids: int32 [12288, 8], P(('dp', 'ep'))
- gate_vals: float32 [12288, 8], P(('dp', 'ep'))
- w_gate: bfloat16 [32, 1024, 512], P('ep')
- w_up: bfloat16 [32, 1024, 512], P('ep')
- w_down: bfloat16 [32, 512, 1024], P('ep')
- grad_out: bfloat16 [12288, 1024], P(('dp', 'ep'))
Outputs:
- output 1: bfloat16 [12288, 1024], P(('dp', 'ep'))
- output 2: bfloat16 [12288, 1024], P(('dp', 'ep'))
- output 3: bfloat16 [32, 1024, 512], P(('dp', 'ep'))
- output 4: bfloat16 [32, 1024, 512], P(('dp', 'ep'))
- output 5: bfloat16 [32, 512, 1024], P(('dp', 'ep'))
All inputs are finite; a program needn't handle non-finite values.
Results may differ from a plain program's by a relative error of at most 0.00104.
Values are sent between devices in bfloat16 or wider.
A program may use at most 768 MiB of HBM per device.

v0:
```python
import jax
import jax.numpy as jnp
from jax import lax
from jax.sharding import PartitionSpec as P


def slot_positions(expert_ids, num_experts, capacity, hot_expert):
    flat_ids = expert_ids.reshape(-1)
    onehot = (flat_ids[:, None] == jnp.arange(num_experts)[None, :]).astype(jnp.int32)
    slot_rank = jnp.sum((jnp.cumsum(onehot, axis=0) - onehot) * onehot, axis=1)
    return jnp.where(flat_ids == hot_expert, num_experts * capacity + slot_rank, flat_ids * capacity + slot_rank)


def scatter_rows(row_vals, buf_pos, buf_rows):
    return jnp.zeros((buf_rows, row_vals.shape[-1]), row_vals.dtype).at[buf_pos].set(row_vals, unique_indices=True)


def expert_forward(in_rows, gate_w, up_w, down_w):
    act_a = jnp.einsum("secd,edf->secf", in_rows, gate_w, preferred_element_type=jnp.float32)
    act_b = jnp.einsum("secd,edf->secf", in_rows, up_w, preferred_element_type=jnp.float32)
    hidden = (act_a * jax.nn.sigmoid(act_a) * act_b).astype(jnp.bfloat16)
    expert_out = jnp.einsum("secf,efd->secd", hidden, down_w, preferred_element_type=jnp.float32).astype(jnp.bfloat16)
    return act_a, act_b, hidden, expert_out


def expert_backward(in_rows, saved_acts, d_out_rows, gate_w, up_w, down_w):
    act_a, act_b, hidden = saved_acts[0], saved_acts[1], saved_acts[2]
    d_hidden = jnp.einsum("secd,efd->secf", d_out_rows, down_w, preferred_element_type=jnp.float32)
    sig_a = jax.nn.sigmoid(act_a)
    d_act_a = (d_hidden * act_b * sig_a * (1.0 + act_a * (1.0 - sig_a))).astype(jnp.bfloat16)
    d_act_b = (d_hidden * act_a * sig_a).astype(jnp.bfloat16)
    d_in_rows = (jnp.einsum("secf,edf->secd", d_act_a, gate_w, preferred_element_type=jnp.float32) + jnp.einsum("secf,edf->secd", d_act_b, up_w, preferred_element_type=jnp.float32)).astype(jnp.bfloat16)
    grad_gate = jnp.einsum("secd,secf->edf", in_rows, d_act_a, preferred_element_type=jnp.float32)
    grad_up = jnp.einsum("secd,secf->edf", in_rows, d_act_b, preferred_element_type=jnp.float32)
    grad_down = jnp.einsum("secf,secd->efd", hidden, d_out_rows, preferred_element_type=jnp.float32)
    return d_in_rows, (grad_gate, grad_up, grad_down)


def solution(mesh):
    group_size = mesh.shape["ep"]
    num_chips = mesh.shape["dp"] * group_size
    tok_spec = P(("dp", "ep"), None)
    w_spec = P("ep", None, None)
    grad_spec = P(("dp", "ep"), None, None)

    def layer_fn(tokens, expert_ids, gate_vals, w_gate, w_up, w_down, grad_out):
        num_experts = w_gate.shape[0]
        tok_dev = tokens.shape[0] // num_chips
        top_k = expert_ids.shape[1]
        capacity = ((2 * tok_dev * top_k + 8 * num_experts - 1) // (8 * num_experts)) * 8
        hot_expert = num_experts // 2
        local_experts = num_experts // group_size
        owner_dev = hot_expert // local_experts
        hot_local = hot_expert % local_experts
        cold_rows = num_experts * capacity

        def device_fn(tok_rows, route_ids, route_gates, gate_w, up_w, down_w, dy_rows):
            row_width = tok_rows.shape[1]
            is_owner = lax.axis_index("ep") == owner_dev
            buf_pos = slot_positions(route_ids, num_experts, capacity, hot_expert)
            tok_rep = jnp.broadcast_to(tok_rows[:, None, :], (tok_dev, top_k, row_width)).reshape(tok_dev * top_k, row_width)
            d_rep = (route_gates[:, :, None] * dy_rows[:, None, :].astype(jnp.float32)).astype(jnp.bfloat16).reshape(tok_dev * top_k, row_width)
            send_x = scatter_rows(tok_rep, buf_pos, cold_rows + tok_dev)
            send_d = scatter_rows(d_rep, buf_pos, cold_rows + tok_dev)
            cold_shape = (group_size, local_experts, capacity, row_width)
            hot_gate = gate_w[hot_local:hot_local + 1]
            hot_up = up_w[hot_local:hot_local + 1]
            hot_down = down_w[hot_local:hot_local + 1]

            cold_x = lax.all_to_all(send_x[:cold_rows].reshape(cold_shape), "ep", 0, 0)
            hot_x = lax.all_gather(send_x[cold_rows:], "ep")[:, None]
            cold_acts = expert_forward(cold_x, gate_w, up_w, down_w)
            hot_acts = expert_forward(hot_x, hot_gate, hot_up, hot_down)
            cold_back = lax.all_to_all(cold_acts[3], "ep", 0, 0).reshape(cold_rows, row_width)
            hot_back = lax.all_to_all(hot_acts[3][:, 0], "ep", 0, 0)[owner_dev]
            y_rows = jnp.concatenate([cold_back, hot_back], axis=0)[buf_pos].reshape(tok_dev, top_k, row_width)
            moe_out = jnp.sum(route_gates[:, :, None] * y_rows.astype(jnp.float32), axis=1).astype(jnp.bfloat16)

            cold_d = lax.all_to_all(send_d[:cold_rows].reshape(cold_shape), "ep", 0, 0)
            hot_d = lax.all_gather(send_d[cold_rows:], "ep")[:, None]
            cold_dx, cold_grads = expert_backward(cold_x, cold_acts, cold_d, gate_w, up_w, down_w)
            hot_dx, hot_grads = expert_backward(hot_x, hot_acts, hot_d, hot_gate, hot_up, hot_down)
            cold_dx_back = lax.all_to_all(cold_dx, "ep", 0, 0).reshape(cold_rows, row_width)
            hot_dx_back = lax.all_to_all(hot_dx[:, 0], "ep", 0, 0)[owner_dev]
            dx_rows = jnp.concatenate([cold_dx_back, hot_dx_back], axis=0)[buf_pos].reshape(tok_dev, top_k, row_width)
            grad_tokens = jnp.sum(dx_rows.astype(jnp.float32), axis=1).astype(jnp.bfloat16)
            grad_list = [cold_g.at[hot_local].add(jnp.where(is_owner, hot_g[0], 0.0)).astype(jnp.bfloat16) for cold_g, hot_g in zip(cold_grads, hot_grads)]
            return moe_out, grad_tokens, grad_list[0], grad_list[1], grad_list[2]

        return jax.shard_map(device_fn, mesh=mesh, in_specs=(tok_spec, tok_spec, tok_spec, w_spec, w_spec, w_spec, tok_spec), out_specs=(tok_spec, tok_spec, grad_spec, grad_spec, grad_spec), check_vma=False)(tokens, expert_ids, gate_vals, w_gate, w_up, w_down, grad_out)

    return layer_fn
```

profile of v0, /device:TPU:97, one launch (start us, length us, event | category | flops | bytes accessed | tf_op | source)
XLA Modules:
  0.0 1610.7 jit_solution(17466782629947148838)
XLA Ops:
  7.3 0.8 broadcast_compare_fusion
  8.8 0.8 copy.29
  10.6 9.2 reduce-window.6
  20.7 22.1 %scatter_custom_fusion = bf16[6528,1024]{1,0:T(8,128)(2,1)} fusion(s32[3072]{0:T(1024)S(1)} %bitcast.315, bf16[]{:T(256)} %constant.79.clone.1, bf16[384,1024]{1,0:T(8,128)(2,1)} %param.13), kind=kCustom, calls=%fused_computation.71 | custom fusion | bytes 14155778 | tf_op jit(solution)/shard_map/scatter | solution.py:15
  42.8 2.1 slice.96
  46.6 23.0 %scatter_custom_fusion.1 = bf16[6528,1024]{1,0:T(8,128)(2,1)} fusion(s32[3072]{0:T(1024)S(1)} %bitcast.316, bf16[]{:T(256)} %constant.79.clone.1, f32[384,1024]{1,0:T(8,128)S(1)} %convert_element_type.110, f32[3072]{0:T(1024)S(1)} %mul.103), kind=kCustom, calls=%fused_computation.69 | custom fusion | flops 6291456 | bytes 14954498 | tf_op jit(solution)/shard_map/scatter | solution.py:15
  69.6 2.1 slice.99
  71.7 10.5 slice.95
  82.2 9.1 all-to-all-start
  91.4 10.5 slice.98
  101.9 171.7 %all-to-all-done = bf16[32,1,192,1024]{3,2,1,0:T(8,128)(2,1)} async-done(((bf16[32,1,192,1024]{3,2,1,0:T(8,128)(2,1)}), bf16[32,1,192,1024]{3,2,1,0:T(8,128)(2,1)}, u32[]{:S(2)}, u32[]{:S(2)}) %all-to-all-start) | async-done | bytes 12582944 | tf_op jit(solution)/shard_map/all_to_all | solution.py:70
  273.5 12.3 all-to-all-start.3
  285.9 14.4 fusion.41
  300.3 14.2 fusion.43
  314.5 161.4 %all-to-all-done.3 = bf16[32,1,192,1024]{3,2,1,0:T(8,128)(2,1)} async-done(((bf16[32,1,192,1024]{3,2,1,0:T(8,128)(2,1)}), bf16[32,1,192,1024]{3,2,1,0:T(8,128)(2,1)}, u32[]{:S(2)}, u32[]{:S(2)}) %all-to-all-start.3) | async-done | bytes 12582944 | tf_op jit(solution)/shard_map/all_to_all | solution.py:79
  475.9 25.5 %fusion.23 = (bf16[32,1,192,512]{3,2,0,1:T(8,128)(2,1)}, bf16[32,1,192,512]{3,2,0,1:T(8,128)(2,1)}, bf16[32,1,192,512]{3,2,0,1:T(8,128)(2,1)S(1)}) fusion(f32[32,192,512]{2,1,0:T(8,128)} %fusion.43, f32[32,192,512]{2,1,0:T(8,128)} %fusion.41, bf16[1,512,1024]{2,1,0:T(8,128)(2,1)S(1)} %copy-done, bf16[32,1,192,1024]{3,2,1,0:T(8,128)(2,1)} %all-to-all-done.3), kind=kOutput, calls=%fused_computation.41 | convolution fusion | flops 6492782592 | bytes 57671680 | tf_op jit(solution)/shard_map/secd,efd->secf/dot_general | solution.py:28
  501.4 2.6 copy-done.11
  504.0 9.7 convert_bitcast_fusion
  513.8 25.2 %all-to-all-start.1 = ((bf16[32,1,192,1024]{3,2,1,0:T(8,128)(2,1)}), bf16[32,1,192,1024]{3,2,1,0:T(8,128)(2,1)}, u32[]{:S(2)}, u32[]{:S(2)}) async-start(bf16[32,1,192,1024]{3,2,1,0:T(8,128)(2,1)} %convert_bitcast_fusion), calls=%async_computation.1 | async-start | bytes 25165824 | tf_op jit(solution)/shard_map/all_to_all | solution.py:74
  539.0 22.5 %fusion.89 = f32[32,384,512]{2,1,0:T(8,128)} fusion(bf16[32,384,1024]{2,1,0:T(8,128)(2,1)} %bitcast.318, bf16[1,1024,512]{2,1,0:T(8,128)(2,1)S(1)} %copy-done.9), kind=kOutput, calls=%fused_computation.104 | convolution fusion | flops 12884901888 | bytes 51380224 | tf_op jit(solution)/shard_map/secd,edf->secf/dot_general | solution.py:20
  561.5 23.0 %fusion.94 = f32[32,384,512]{2,1,0:T(8,128)} fusion(bf16[32,384,1024]{2,1,0:T(8,128)(2,1)} %bitcast.319, bf16[1,1024,512]{2,1,0:T(8,128)(2,1)S(1)} %copy-done.8), kind=kOutput, calls=%fused_computation.109 | convolution fusion | flops 12884901888 | bytes 51380224 | tf_op jit(solution)/shard_map/secd,edf->secf/dot_general | solution.py:19
  584.4 42.5 %fusion.4 = (bf16[32,1,384,512]{3,2,0,1:T(8,128)(2,1)}, bf16[32,1,384,512]{3,2,0,1:T(8,128)(2,1)}, bf16[32,1,384,512]{3,2,0,1:T(8,128)(2,1)}) fusion(f32[32,384,512]{2,1,0:T(8,128)} %fusion.94, f32[32,384,512]{2,1,0:T(8,128)} %fusion.89, bf16[32,384,1024]{2,1,0:T(8,128)(2,1)} %bitcast.322, bf16[1,512,1024]{2,1,0:T(8,128)(2,1)S(1)} %copy-done), kind=kOutput, calls=%fused_computation.11 | convolution fusion | flops 12985565184 | bytes 114294784 | tf_op jit(solution)/shard_map/secd,efd->secf/dot_general | solution.py:28
  627.0 21.4 %convolution_convert_fusion = bf16[32,384,1024]{2,1,0:T(8,128)(2,1)} fusion(bf16[32,1,384,512]{3,2,0,1:T(8,128)(2,1)} %get-tuple-element.43, bf16[1,512,1024]{2,1,0:T(8,128)(2,1)S(1)} %copy-done), kind=kOutput, calls=%fused_computation.22 | convolution fusion | flops 12897484800 | bytes 38797312 | tf_op jit(solution)/shard_map/secf,efd->secd/dot_general | solution.py:22
  648.4 46.9 %all-to-all-done.1 = bf16[32,1,192,1024]{3,2,1,0:T(8,128)(2,1)} async-done(((bf16[32,1,192,1024]{3,2,1,0:T(8,128)(2,1)}), bf16[32,1,192,1024]{3,2,1,0:T(8,128)(2,1)}, u32[]{:S(2)}, u32[]{:S(2)}) %all-to-all-start.1) | async-done | bytes 12582944 | tf_op jit(solution)/shard_map/all_to_all | solution.py:74
  695.2 19.0 %all-to-all-start.2 = ((bf16[32,384,1024]{2,1,0:T(8,128)(2,1)}), bf16[32,384,1024]{2,1,0:T(8,128)(2,1)}, u32[]{:S(2)}, u32[]{:S(2)}) async-start(bf16[32,384,1024]{2,1,0:T(8,128)(2,1)} %convolution_convert_fusion), calls=%async_computation.2 | async-start | bytes 50331648 | tf_op jit(solution)/shard_map/all_to_all | solution.py:75
  714.3 24.6 %fusion.17 = f32[32,384,1024]{2,1,0:T(8,128)} fusion(bf16[32,1,384,512]{3,2,0,1:T(8,128)(2,1)} %get-tuple-element.42, bf16[1,1024,512]{2,1,0:T(8,128)(2,1)S(1)} %copy-done.8), kind=kOutput, calls=%fused_computation.33 | convolution fusion | flops 12884901888 | bytes 63963136 | tf_op jit(solution)/shard_map/secf,edf->secd/dot_general | solution.py:32
  738.9 29.8 %add_convert_fusion = bf16[32,384,1024]{2,1,0:T(8,128)(2,1)} fusion(f32[32,384,1024]{2,1,0:T(8,128)} %fusion.17, bf16[32,1,384,512]{3,2,0,1:T(8,128)(2,1)} %get-tuple-element.41, bf16[1,1024,512]{2,1,0:T(8,128)(2,1)S(1)} %copy-done.10), kind=kOutput, calls=%fused_computation.4 | convolution fusion | flops 12910067712 | bytes 89128960 | tf_op jit(solution)/shard_map/secf,edf->secd/dot_general | solution.py:32
  768.7 251.2 %all-to-all-done.2 = bf16[32,384,1024]{2,1,0:T(8,128)(2,1)} async-done(((bf16[32,384,1024]{2,1,0:T(8,128)(2,1)}), bf16[32,384,1024]{2,1,0:T(8,128)(2,1)}, u32[]{:S(2)}, u32[]{:S(2)}) %all-to-all-start.2) | async-done | bytes 25165856 | tf_op jit(solution)/shard_map/all_to_all | solution.py:75
  1019.8 41.3 %all-to-all-start.5 = ((bf16[32,384,1024]{2,1,0:T(8,128)(2,1)}), bf16[32,384,1024]{2,1,0:T(8,128)(2,1)}, u32[]{:S(2)}, u32[]{:S(2)}) async-start(bf16[32,384,1024]{2,1,0:T(8,128)(2,1)} %add_convert_fusion), calls=%async_computation.5 | async-start | bytes 50331648 | tf_op jit(solution)/shard_map/all_to_all | solution.py:84
  1061.1 14.6 fusion.53
  1075.7 16.2 %fusion.10 = bf16[32,1,192,1024]{3,2,1,0:T(8,128)(2,1)} fusion(f32[32,192,1024]{2,1,0:T(8,128)} %fusion.53, bf16[32,1,192,512]{3,2,0,1:T(8,128)(2,1)} %get-tuple-element.44, bf16[1,1024,512]{2,1,0:T(8,128)(2,1)S(1)} %copy-done.10), kind=kOutput, calls=%fused_computation.25 | convolution fusion | flops 6455033856 | bytes 45088768 | tf_op jit(solution)/shard_map/secf,edf->secd/dot_general | solution.py:32
  1091.9 277.4 %all-to-all-done.5 = bf16[32,384,1024]{2,1,0:T(8,128)(2,1)} async-done(((bf16[32,384,1024]{2,1,0:T(8,128)(2,1)}), bf16[32,384,1024]{2,1,0:T(8,128)(2,1)}, u32[]{:S(2)}, u32[]{:S(2)}) %all-to-all-start.5) | async-done | bytes 25165856 | tf_op jit(solution)/shard_map/all_to_all | solution.py:84
  1369.3 33.8 %all-to-all-start.4 = ((bf16[32,1,192,1024]{3,2,1,0:T(8,128)(2,1)}), bf16[32,1,192,1024]{3,2,1,0:T(8,128)(2,1)}, u32[]{:S(2)}, u32[]{:S(2)}) async-start(bf16[32,1,192,1024]{3,2,1,0:T(8,128)(2,1)} %fusion.10), calls=%async_computation.4 | async-start | bytes 25165824 | tf_op jit(solution)/shard_map/all_to_all | solution.py:83
  1403.2 11.6 fusion.37
  1414.8 11.6 fusion.39
  1426.5 9.7 fusion.25
  1436.2 21.2 %fusion.79 = bf16[1,512,1024]{2,1,0:T(8,128)(2,1)} fusion(bf16[32,384,1024]{2,1,0:T(8,128)(2,1)} %bitcast.323, bf16[32,1,384,512]{3,2,0,1:T(8,128)(2,1)} %get-tuple-element.43, f32[512,1024,1]{1,0,2:T(8,128)S(1)} %fusion.25, pred[]{:T(512)S(6)} %eq.55), kind=kOutput, calls=%fused_computation.96 | convolution fusion | flops 12886474752 | bytes 40894464 | tf_op jit(solution)/shard_map/secf,secd->efd/dot_general | solution.py:35
  1457.4 21.2 %fusion.73 = bf16[1,1024,512]{2,1,0:T(8,128)(2,1)} fusion(bf16[32,384,1024]{2,1,0:T(8,128)(2,1)} %bitcast.320, bf16[32,1,384,512]{3,2,0,1:T(8,128)(2,1)} %get-tuple-element.42, f32[1024,512,1]{1,0,2:T(8,128)S(1)} %fusion.39, pred[]{:T(512)S(6)} %eq.55), kind=kOutput, calls=%fused_computation.94 | convolution fusion | flops 12886474752 | bytes 40894464 | tf_op jit(solution)/shard_map/secd,secf->edf/dot_general | solution.py:33
  1478.6 21.0 %fusion.76 = bf16[1,1024,512]{2,1,0:T(8,128)(2,1)} fusion(bf16[32,384,1024]{2,1,0:T(8,128)(2,1)} %bitcast.321, bf16[32,1,384,512]{3,2,0,1:T(8,128)(2,1)} %get-tuple-element.41, f32[1024,512,1]{1,0,2:T(8,128)S(1)} %fusion.37, pred[]{:T(512)S(6)} %eq.55), kind=kOutput, calls=%fused_computation.95 | convolution fusion | flops 12886474752 | bytes 40894464 | tf_op jit(solution)/shard_map/secd,secf->edf/dot_general | solution.py:34
  1499.6 1.2 slice_bitcast_fusion.1
  1500.8 16.5 %pad_maximum_fusion = bf16[6528,1024]{1,0:T(8,128)(2,1)} fusion(bf16[384,1024]{1,0:T(8,128)(2,1)S(1)} %slice_bitcast_fusion.1, bf16[6144,1024]{1,0:T(8,128)(2,1)} %bitcast.27), kind=kLoop, calls=%fused_computation.23 | loop fusion | flops 26738688 | bytes 26738688 | tf_op jit(solution)/shard_map/concatenate | solution.py:76
  1517.3 22.4 %gather_fusion = bf16[3072,1024]{1,0:T(8,128)(2,1)} fusion(bf16[6528,1024]{1,0:T(8,128)(2,1)} %pad_maximum_fusion, s32[3072]{0:T(1024)S(1)} %broadcast_clamp_fusion), kind=kCustom, calls=%fused_computation | custom fusion | bytes 12595200 | tf_op jit(solution)/shard_map/gather | solution.py:76
  1539.7 1.2 slice_bitcast_fusion
  1540.9 7.6 fusion.11
  1548.5 6.7 all-to-all-done.4
  1555.3 16.5 %pad_maximum_fusion.1 = bf16[6528,1024]{1,0:T(8,128)(2,1)} fusion(bf16[384,1024]{1,0:T(8,128)(2,1)S(1)} %slice_bitcast_fusion, bf16[6144,1024]{1,0:T(8,128)(2,1)} %bitcast.56), kind=kLoop, calls=%fused_computation.24 | loop fusion | flops 26738688 | bytes 26738688 | tf_op jit(solution)/shard_map/concatenate | solution.py:85
  1571.8 22.5 %gather_fusion.1 = bf16[3072,1024]{1,0:T(8,128)(2,1)} fusion(bf16[6528,1024]{1,0:T(8,128)(2,1)} %pad_maximum_fusion.1, s32[3072]{0:T(1024)S(1)} %broadcast_clamp_fusion), kind=kCustom, calls=%fused_computation.1 | custom fusion | bytes 12595200 | tf_op jit(solution)/shard_map/gather | solution.py:85
  1594.4 9.0 bitcast_reduce_fusion
  (52 shorter events, 4.4 us)
Async XLA Ops:
  7.2 468.7 %copy-start = (bf16[1,512,1024]{2,1,0:T(8,128)(2,1)S(1)}, bf16[1,512,1024]{2,1,0:T(8,128)(2,1)}, u32[]{:S(2)}) copy-start(bf16[1,512,1024]{2,1,0:T(8,128)(2,1)} %param.18) | copy-start | bytes 3145732
  7.2 38.3 %copy-start.7 = (f32[384,8]{0,1:T(8,128)S(1)}, f32[384,8]{0,1:T(8,128)}, u32[]{:S(2)}) copy-start(f32[384,8]{0,1:T(8,128)} %param.15) | copy-start | bytes 36868
  7.2 39.3 %copy-start.4 = (bf16[384,1024]{1,0:T(8,128)(2,1)S(1)}, bf16[384,1024]{1,0:T(8,128)(2,1)}, u32[]{:S(2)}) copy-start(bf16[384,1024]{1,0:T(8,128)(2,1)} %param.19) | copy-start | bytes 2359300
  7.2 531.7 %all-gather.5.cloned.1.call-start = ((), (), s32[]{:S(2)}) async-start(), calls=%async_computation.6 | async-start | bytes 25952256 | tf_op jit(solution)/shard_map/all_gather | solution.py:71
  20.7 48.9 %copy-start.5 = (s32[3072,1]{0,1:T(1,128)}, s32[3072,1]{0,1:T(1,128)S(1)}, u32[]{:S(2)}) copy-start(s32[3072,1]{0,1:T(1,128)S(1)} %compare_select_fusion) | copy-start | bytes 36868
  45.0 539.5 %all-gather.7.cloned.1.call-start = ((), (), s32[]{:S(2)}) async-start(), calls=%async_computation.7 | async-start | bytes 25952256 | tf_op jit(solution)/shard_map/all_gather | solution.py:80
  45.6 0.7 copy-start.2
  82.2 191.3 %all-to-all-start = ((bf16[32,1,192,1024]{3,2,1,0:T(8,128)(2,1)}), bf16[32,1,192,1024]{3,2,1,0:T(8,128)(2,1)}, u32[]{:S(2)}, u32[]{:S(2)}) async-start(bf16[32,1,192,1024]{3,2,1,0:T(8,128)(2,1)} %bitcast.310), calls=%async_computation | async-start | bytes 25165824 | tf_op jit(solution)/shard_map/all_to_all | solution.py:70
  273.5 12.3 copy-start.9
  273.5 202.4 %all-to-all-start.3 = ((bf16[32,1,192,1024]{3,2,1,0:T(8,128)(2,1)}), bf16[32,1,192,1024]{3,2,1,0:T(8,128)(2,1)}, u32[]{:S(2)}, u32[]{:S(2)}) async-start(bf16[32,1,192,1024]{3,2,1,0:T(8,128)(2,1)} %bitcast.309), calls=%async_computation.3 | async-start | bytes 25165824 | tf_op jit(solution)/shard_map/all_to_all | solution.py:79
  285.9 14.4 copy-start.8
  501.4 2.6 copy-start.11
  513.8 181.5 %all-to-all-start.1 = ((bf16[32,1,192,1024]{3,2,1,0:T(8,128)(2,1)}), bf16[32,1,192,1024]{3,2,1,0:T(8,128)(2,1)}, u32[]{:S(2)}, u32[]{:S(2)}) async-start(bf16[32,1,192,1024]{3,2,1,0:T(8,128)(2,1)} %convert_bitcast_fusion), calls=%async_computation.1 | async-start | bytes 25165824 | tf_op jit(solution)/shard_map/all_to_all | solution.py:74
  695.2 324.6 %all-to-all-start.2 = ((bf16[32,384,1024]{2,1,0:T(8,128)(2,1)}), bf16[32,384,1024]{2,1,0:T(8,128)(2,1)}, u32[]{:S(2)}, u32[]{:S(2)}) async-start(bf16[32,384,1024]{2,1,0:T(8,128)(2,1)} %convolution_convert_fusion), calls=%async_computation.2 | async-start | bytes 50331648 | tf_op jit(solution)/shard_map/all_to_all | solution.py:75
  714.3 24.6 %copy-start.10 = (bf16[1,1024,512]{2,1,0:T(8,128)(2,1)S(1)}, bf16[1,1024,512]{2,1,0:T(8,128)(2,1)}, u32[]{:S(2)}) copy-start(bf16[1,1024,512]{2,1,0:T(8,128)(2,1)} %param.17) | copy-start | bytes 3145732
  768.7 292.5 %copy-start.6 = (s32[3072,1]{0,1:T(1,128)S(1)}, s32[3072,1]{0,1:T(1,128)}, u32[]{:S(2)}) copy-start(s32[3072,1]{0,1:T(1,128)} %copy-done.5) | copy-start | bytes 36868
  1019.8 349.5 %all-to-all-start.5 = ((bf16[32,384,1024]{2,1,0:T(8,128)(2,1)}), bf16[32,384,1024]{2,1,0:T(8,128)(2,1)}, u32[]{:S(2)}, u32[]{:S(2)}) async-start(bf16[32,384,1024]{2,1,0:T(8,128)(2,1)} %add_convert_fusion), calls=%async_computation.5 | async-start | bytes 50331648 | tf_op jit(solution)/shard_map/all_to_all | solution.py:84
  1369.3 186.0 %all-to-all-start.4 = ((bf16[32,1,192,1024]{3,2,1,0:T(8,128)(2,1)}), bf16[32,1,192,1024]{3,2,1,0:T(8,128)(2,1)}, u32[]{:S(2)}, u32[]{:S(2)}) async-start(bf16[32,1,192,1024]{3,2,1,0:T(8,128)(2,1)} %fusion.10), calls=%async_computation.4 | async-start | bytes 25165824 | tf_op jit(solution)/shard_map/all_to_all | solution.py:83
  1403.1 23.3 %slice-start = ((s8[6291456]{0:T(1024)(128)(4,1)}), s8[4194304]{0:T(1024)(128)(4,1)S(1)}, s32[]{:S(2)}) async-start(s8[6291456]{0:T(1024)(128)(4,1)} %bitcast.324), calls=%async_computation.8 | async-start | bytes 8388608
  1414.8 11.7 slice-start.1
  1517.3 23.6 %copy-start.3 = (f32[384,8]{1,0:T(8,128)S(1)}, f32[384,8]{1,0:T(8,128)}, u32[]{:S(2)}) copy-start(f32[384,8]{1,0:T(8,128)} %copy-done.2) | copy-start | bytes 36868
  1571.8 31.6 %copy-start.1 = (bf16[1,512,1024]{2,1,0:T(8,128)(2,1)S(1)}, bf16[1,512,1024]{2,1,0:T(8,128)(2,1)}, u32[]{:S(2)}) copy-start(bf16[1,512,1024]{2,1,0:T(8,128)(2,1)} %param.18) | copy-start | bytes 3145732
Sparse Core Ops, SparseCore 0:
  45.1 221.0 all-gather.4
  268.9 215.2 all-gather.6
where the time goes:
time: 1630 us; the launch traced here: 1610 us
  waiting for transfers between devices  915 us (56%)
  matrix products  355 us (22%)
  starting transfers between devices  141 us (9%)
  local copies, waits for them, and re-layouts  100 us (6%)
  other arithmetic  84.1 us (5%)
    all_to_all x1, waiting for transfers between devices, device_fn(): hot_dx_back = lax.all_to_all(hot_dx[:, 0], 'ep', 0, 0)[owner_dev]  277 us
    all_to_all x1, waiting for transfers between devices, device_fn(): hot_back = lax.all_to_all(hot_acts[3][:, 0], 'ep', 0, 0)[owner_dev]  251 us
    all_to_all x1, waiting for transfers between devices, device_fn(): cold_x = lax.all_to_all(send_x[:cold_rows].reshape(cold_shape), 'ep', 0, 0)  172 us
    all_to_all x1, waiting for transfers between devices, device_fn(): cold_d = lax.all_to_all(send_d[:cold_rows].reshape(cold_shape), 'ep', 0, 0)  161 us
    dot_general x2, matrix products, expert_backward(): jnp.einsum('secd,efd->secf', d_out_rows, down_w, preferred_element_type=j...  68 us
    all_to_all x1, waiting for transfers between devices, device_fn(): lax.all_to_all(cold_acts[3], 'ep', 0, 0).reshape(cold_rows, row_width)  46.9 us
    dot_general x2, matrix products, expert_backward(): jnp.einsum('secf,edf->secd', d_act_b, up_w, preferred_element_type=jnp.fl...  46 us
    all_to_all x1, starting transfers between devices, device_fn(): hot_dx_back = lax.all_to_all(hot_dx[:, 0], 'ep', 0, 0)[owner_dev]  41.3 us
  transfers between devices with their start and end apart: 8, of which 6 were waited for; matrix products, arithmetic and copies ran while one was open for 28% of the time, Pallas kernels for 0%

commit v1 on v0

v1 whole, which is shorter than its diff:
```python
import functools
import math

import jax
import jax.numpy as jnp
from jax import lax
from jax.experimental import pallas as pl
from jax.experimental.pallas import tpu as pltpu
from jax.sharding import PartitionSpec as P

MESH = pl.DeviceIdType.MESH
F32 = jnp.float32
BF16 = jnp.bfloat16
NT = (((1,), (1,)), ((), ()))
NUM_COPIES = 120


def dot(lhs, rhs):
    return jnp.dot(lhs, rhs, preferred_element_type=F32)


def dot_nt(lhs, rhs):
    return lax.dot_general(lhs, rhs, NT, preferred_element_type=F32)


def gate_columns(gate_row, width):
    cols = jnp.transpose(jnp.broadcast_to(gate_row, (128, gate_row.shape[1])))
    return jnp.concatenate([cols] * (width // 128), axis=1)


def layer_kernel(side, x_ref, dy_ref, g_ref, w1_ref, w3_ref, w2_ref,
                 y_out, dx_out, dw1_out, dw3_out, dw2_out, xg, dg, gg, wg, rs_full,
                 wv, xrow, dyrow, grow, acc, rs_half, dw, xs, ds, gs, u_s, dab_s, do_s, xt_s,
                 send_sem, recv_sem, loc_sem):
    rows, width = x_ref.shape
    ff = w1_ref.shape[1]
    half = rows // 2
    fc = ff // 2
    nc = width // 4
    me = lax.axis_index("ep")
    core = lax.rem(me, 2)
    px = lax.rem(me // 2, side)
    py = me // (2 * side)

    def dev(yy, xx, cc):
        return (lax.rem(yy + side, side) * side + lax.rem(xx + side, side)) * 2 + cc

    xp, xm = dev(py, px + 1, core), dev(py, px - 1, core)
    yp, ym = dev(py + 1, px, core), dev(py - 1, px, core)
    partner = dev(py, px, 1 - core)

    copies = {}

    def reg(key, src, dst, target):
        k = len(copies)
        copies[key] = pltpu.make_async_remote_copy(
            src_ref=src, dst_ref=dst, send_sem=send_sem.at[k], recv_sem=recv_sem.at[k],
            device_id={"ep": target}, device_id_type=MESH)

    def reg_ring(key, plus, minus, src, buf, n):
        reg(key + ("+",), src, buf(2), plus)
        reg(key + ("-",), src, buf(1), minus)
        reg(key + ("2+",), buf(2).at[pl.ds(0, n // 2)], buf(3).at[pl.ds(0, n // 2)], plus)
        reg(key + ("2-",), buf(1).at[pl.ds(n // 2, n // 2)], buf(3).at[pl.ds(n // 2, n // 2)], minus)

    wn = wv.shape[1]
    reg_ring(("w",), yp, ym, wv.at[0], lambda s: wg.at[{1: 2, 2: 3, 3: 6}[s]], wn)
    reg(("wp", 0), wv.at[0], wg.at[1], partner)
    reg(("wp", 2), wg.at[2], wg.at[4], partner)
    reg(("wp", 3), wg.at[3], wg.at[5], partner)
    reg(("wp", 6), wg.at[6], wg.at[7], partner)
    for name, own, buf, n in (("x", x_ref, xg, rows), ("g", g_ref, gg, g_ref.shape[0])):
        reg_ring((name, 0), xp, xm, own, lambda s, buf=buf: buf.at[0, s, 0], n)
        for i in range(4):
            src = own if i == 0 else buf.at[0, i, 0]
            reg_ring((name, "y", i), yp, ym, src, lambda s, buf=buf, i=i: buf.at[s, i, 0], n)
    reg_ring(("d", "y"), yp, ym, dy_ref, lambda s: dg.at[s, 0, 0], rows)
    for j in range(4):
        src = dy_ref if j == 0 else dg.at[j, 0, 0]
        reg_ring(("d", j), xp, xm, src, lambda s, j=j: dg.at[j, s, 0], rows)
    for name, own, buf in (("x", x_ref, xg), ("g", g_ref, gg), ("d", dy_ref, dg)):
        for j in range(4):
            for i in range(4):
                reg((name + "p", j, i), own if (i, j) == (0, 0) else buf.at[j, i, 0], buf.at[j, i, 1], partner)
    reg(("r", "h+"), acc.at[3, :, pl.ds(0, half)], rs_half.at[0], xp)
    reg(("r", "h-"), acc.at[3, :, pl.ds(half, half)], rs_half.at[1], xm)
    reg(("r", "+"), acc.at[1], rs_full.at[0], xp)
    reg(("r", "-"), acc.at[2], rs_full.at[1], xm)

    def start(*keys):
        for key in keys:
            copies[key].start()

    def arrived(*keys):
        for key in keys:
            copies[key].wait_recv()

    def share(names, j, i):
        start(*[(name + "p", j, i) for name in names])

    def local(src, dst, k):
        return pltpu.make_async_copy(src, dst, loc_sem.at[k])

    w_loads = [local(w1_ref, wv.at[0, pl.ds(0, width), pl.ds(0, ff)], 0),
               local(w3_ref, wv.at[0, pl.ds(0, width), pl.ds(ff, ff)], 1),
               local(w2_ref, wv.at[0, pl.ds(width, ff)], 2)]
    t_loads = [local(x_ref, xrow.at[0], 3), local(dy_ref, dyrow.at[0], 4), local(g_ref, grow.at[0], 5)]
    for c in w_loads + t_loads:
        c.start()

    barrier = pltpu.get_barrier_semaphore()
    for target in (xp, xm, yp, ym, partner):
        pl.semaphore_signal(barrier, inc=1, device_id={"ep": target}, device_id_type=MESH)
    pl.semaphore_wait(barrier, 5)

    for name in ("g", "x", "d"):
        start((name, 0, "+"), (name, 0, "-"))
    for c in w_loads:
        c.wait()
    start(("w", "+"), ("w", "-"), ("wp", 0), ("d", "y", "+"), ("d", "y", "-"))
    share("gxd", 0, 0)
    for c in t_loads:
        c.wait()
    own_stores = [local(xrow.at[0], xg.at[0, 0, 0], 3), local(dyrow.at[0], dg.at[0, 0, 0], 4),
                  local(grow.at[0], gg.at[0, 0, 0], 5)]
    for c in own_stores:
        c.start()
    for b in range(4):
        for v in range(2):
            acc[b, v] = jnp.zeros((rows, width), F32)
    dw[...] = jnp.zeros_like(dw)

    def stage_row(i, k):
        return [local(xg.at[0, i, 0], xrow.at[i], k), local(dg.at[0, i, 0], dyrow.at[i], k + 1),
                local(gg.at[0, i, 0], grow.at[i], k + 2)]

    def stage_w(e, slot):
        return local(wg.at[e], wv.at[slot], 6 + slot)

    def acts(x, do, slot, h):
        a = dot(x, wv[slot, pl.ds(0, width), pl.ds(h * fc, fc)])
        b = dot(x, wv[slot, pl.ds(0, width), pl.ds(ff + h * fc, fc)])
        du = dot_nt(do, wv[slot, pl.ds(width + h * fc, fc), :])
        sig = jax.nn.sigmoid(a)
        hidden = a * sig * b
        da = du * b * sig * (1.0 + a * (1.0 - sig))
        db = du * a * sig
        return hidden, da, db

    def row_step(slot, i, jrel, plane):
        expert = dev(py + jrel, px, lax.rem(core + plane, 2))
        gate = gate_columns(grow[i, pl.ds(expert, 1), :], nc)
        routed = gate > 0.0
        for n in range(4):
            cols = pl.ds(n * nc, nc)
            do_s[pl.ds(0, rows), cols] = (gate * dyrow[i, :, cols].astype(F32)).astype(BF16)
        for h in range(2):
            hidden, da, db = acts(xrow[i], do_s[pl.ds(0, rows), :], slot, h)
            u_s[pl.ds(0, rows), pl.ds(h * fc, fc)] = hidden.astype(BF16)
            dab_s[pl.ds(0, rows), pl.ds(h * fc, fc)] = da.astype(BF16)
            dab_s[pl.ds(0, rows), pl.ds(ff + h * fc, fc)] = db.astype(BF16)
        for n in range(4):
            cols = pl.ds(n * nc, nc)
            o = dot(u_s[pl.ds(0, rows), :], wv[slot, pl.ds(width, ff), cols]).astype(BF16).astype(F32)
            acc[i, 0, :, cols] += jnp.where(routed, gate * o, 0.0)
            dxp = dot_nt(dab_s[pl.ds(0, rows), :], wv[slot, pl.ds(n * nc, nc), :]).astype(BF16).astype(F32)
            acc[i, 1, :, cols] += jnp.where(routed, dxp, 0.0)

    def first_steps(s, carry):
        i, e = s // 2, lax.rem(s, 2)

        @pl.when(s == 1)
        def _():
            arrived(("wp", 0))
            c = stage_w(1, 1)
            c.start()
            c.wait()

        @pl.when(s == 2)
        def _():
            for name in ("g", "x", "d"):
                arrived((name, 0, "+"), (name, 0, "-"))
                start((name, 0, "2+"), (name, 0, "2-"))
            share("gxd", 0, 1)
            share("gxd", 0, 2)
            cs = stage_row(1, 9) + stage_row(2, 12)
            for c in cs:
                c.start()
            for c in cs:
                c.wait()

        @pl.when(s == 6)
        def _():
            for name in ("g", "x", "d"):
                arrived((name, 0, "2+"), (name, 0, "2-"))
            share("gxd", 0, 3)
            cs = stage_row(3, 9)
            for c in cs:
                c.start()
            for c in cs:
                c.wait()

        row_step(e, i, 0, e)
        return carry

    lax.fori_loop(0, 8, first_steps, 0)

    arrived(("w", "+"), ("w", "-"))
    start(("w", "2+"), ("w", "2-"), ("wp", 2), ("wp", 3))
    stage_w(2, 2).start()

    def middle_steps(s, carry):
        k, i = s // 4, lax.rem(s, 4)
        slot = 2 - lax.rem(k, 2)

        @pl.when(i == 0)
        def _():
            stage_w(2, slot).wait()

        @pl.when(i == 3)
        def _():
            @pl.when(k == 0)
            def _():
                stage_w(3, 1).start()

            @pl.when(k == 1)
            def _():
                arrived(("wp", 2))
                stage_w(4, 2).start()

            @pl.when(k == 2)
            def _():
                arrived(("wp", 3))
                stage_w(5, 1).start()

            @pl.when(k == 3)
            def _():
                arrived(("w", "2+"), ("w", "2-"))
                start(("wp", 6))
                stage_w(6, 2).start()

        @pl.when(s == 2)
        def _():
            arrived(("d", "y", "+"), ("d", "y", "-"))
            start(("d", "y", "2+"), ("d", "y", "2-"))
            for j in (1, 2):
                start(("d", j, "+"), ("d", j, "-"))
                share("d", j, 0)
            for b in range(4):
                for name in ("g", "x"):
                    start((name, "y", b, "+"), (name, "y", b, "-"))

        @pl.when(s == 9)
        def _():
            arrived(("d", "y", "2+"), ("d", "y", "2-"))
            start(("d", 3, "+"), ("d", 3, "-"))
            share("d", 3, 0)

        for j, when in ((1, 11), (2, 14)):
            @pl.when(s == when)
            def _(j=j):
                arrived(("d", j, "+"), ("d", j, "-"))
                start(("d", j, "2+"), ("d", j, "2-"))
                share("d", j, 1)
                share("d", j, 2)

        row_step(slot, i, 1 + 2 * lax.rem(k, 2), k // 2)
        return carry

    lax.fori_loop(0, 16, middle_steps, 0)
    stage_w(6, 2).wait()

    def pass_on_x(b):
        for name in ("g", "x"):
            arrived((name, "y", b, "+"), (name, "y", b, "-"))
            start((name, "y", b, "2+"), (name, "y", b, "2-"))
        share("gx", 1, b)
        share("gx", 2, b)

    def last_steps(s, carry):
        i, e = 3 - s // 2, lax.rem(s, 2)

        @pl.when(s == 1)
        def _():
            arrived(("wp", 6))
            c = stage_w(7, 1)
            c.start()
            c.wait()

        @pl.when(s == 2)
        def _():
            start(("r", "h+"), ("r", "h-"))
            pass_on_x(0)

        @pl.when(s == 4)
        def _():
            arrived(("d", 3, "+"), ("d", 3, "-"))
            start(("d", 3, "2+"), ("d", 3, "2-"))
            share("d", 3, 1)
            share("d", 3, 2)
            pass_on_x(1)

        @pl.when(s == 6)
        def _():
            arrived(("r", "h+"), ("r", "h-"))
            acc[1, :, pl.ds(0, half), :] += rs_half[0]
            acc[2, :, pl.ds(half, half), :] += rs_half[1]
            start(("r", "+"), ("r", "-"))
            pass_on_x(2)

        row_step(2 - e, i, 2, e)
        return carry

    lax.fori_loop(0, 8, last_steps, 0)
    for c in own_stores:
        c.wait()

    def stage_pair(j, i, slot):
        return [local(xg.at[j, i], xs.at[slot], 9 + slot), local(dg.at[j, i], ds.at[slot], 11 + slot),
                local(gg.at[j, i], gs.at[slot], 13 + slot)]

    def get_pair(j, i):
        arrived(("xp", j, i), ("gp", j, i), ("dp", j, i))

    def grad_step(slot):
        gate = jnp.concatenate([gate_columns(gs[slot, p, pl.ds(me, 1), :], nc) for p in range(2)], axis=0)
        x = xs[slot].reshape(2 * rows, width)
        routed = gate[:, :fc] > 0.0 if nc >= fc else jnp.concatenate([gate] * (fc // nc), axis=1) > 0.0
        for n in range(4):
            cols = pl.ds(n * nc, nc)
            dy = ds[slot, :, :, cols].reshape(2 * rows, nc)
            do_s[:, cols] = (gate * dy.astype(F32)).astype(BF16)
        for h in range(2):
            hidden, da, db = acts(x, do_s[...], 0, h)
            u_s[:, pl.ds(h * fc, fc)] = jnp.where(routed, hidden, 0.0).astype(BF16)
            dab_s[:, pl.ds(h * fc, fc)] = jnp.where(routed, da, 0.0).astype(BF16)
            dab_s[:, pl.ds(ff + h * fc, fc)] = jnp.where(routed, db, 0.0).astype(BF16)
        xt_s[pl.ds(0, width), :] = jnp.transpose(x)
        xt_s[pl.ds(width, ff), :] = jnp.transpose(u_s[...])
        for n in range(4):
            cols = pl.ds(n * nc, nc)
            dw[pl.ds(0, width), cols] += dot(xt_s[pl.ds(0, width), :], dab_s[:, cols])
            dw[pl.ds(width, ff), cols] += dot(xt_s[pl.ds(width, ff), :], do_s[:, cols])

    get_pair(0, 0)
    for c in stage_pair(0, 0, 0):
        c.start()

    def grad_steps(q, carry):
        slot = lax.rem(q, 2)
        nxt = q + 1
        nj, ni = nxt // 4, lax.rem(nxt, 4)

        @pl.when(q == 0)
        def _():
            pass_on_x(3)

        for step in range(1, 16):
            j, i = step // 4, step % 4

            @pl.when(q == step - 1)
            def _(j=j, i=i):
                if j == 1 and i == 0:
                    for jj in (1, 2, 3):
                        arrived(("d", jj, "2+"), ("d", jj, "2-"))
                        share("d", jj, 3)
                if j == 2:
                    for name in ("g", "x"):
                        arrived((name, "y", i, "2+"), (name, "y", i, "2-"))
                    share("gx", 3, i)
                get_pair(j, i)

        @pl.when(q < 15)
        def _():
            for c in stage_pair(nj, ni, 1 - slot):
                c.start()

        for c in stage_pair(0, 0, slot):
            c.wait()
        grad_step(slot)
        return carry

    lax.fori_loop(0, 16, grad_steps, 0)

    outs = []
    wv[1] = dw[...].astype(BF16)
    outs += [local(wv.at[1, pl.ds(0, width), pl.ds(0, ff)], dw1_out, 0),
             local(wv.at[1, pl.ds(0, width), pl.ds(ff, ff)], dw3_out, 1),
             local(wv.at[1, pl.ds(width, ff)], dw2_out, 2)]
    for c in outs:
        c.start()
    arrived(("r", "+"), ("r", "-"))
    copies[("r", "+")].wait_send()
    copies[("r", "-")].wait_send()
    fetch = [local(rs_full.at[0], acc.at[1], 3), local(rs_full.at[1], acc.at[2], 4)]
    for c in fetch:
        c.start()
    for c in fetch:
        c.wait()
    for v, (buf, out) in enumerate(((xrow, y_out), (dyrow, dx_out))):
        buf[1] = (acc[0, v] + acc[1, v] + acc[2, v]).astype(BF16)
        c = local(buf.at[1], out, 3 + v)
        c.start()
        outs.append(c)
    for key, c in copies.items():
        if key not in (("r", "+"), ("r", "-")):
            c.wait_send()
    for c in outs:
        c.wait()


def solution(mesh):
    group_size = mesh.shape["ep"]
    side = math.isqrt(group_size // 2)
    tok_spec = P(("dp", "ep"), None)
    w_spec = P("ep", None, None)
    grad_spec = P(("dp", "ep"), None, None)

    def device_fn(x, ids, gates, w1, w3, w2, dy):
        rows, width = x.shape
        ff = w1.shape[2]
        experts = group_size * w1.shape[0]
        onehot = ids[None, :, :] == jnp.arange(experts, dtype=ids.dtype)[:, None, None]
        gate_t = jnp.sum(jnp.where(onehot, gates[None, :, :], 0.0), axis=2)
        any_spec = pl.BlockSpec(memory_space=pl.ANY)
        sds = jax.ShapeDtypeStruct
        out_shape = (
            sds((rows, width), BF16), sds((rows, width), BF16),
            sds((width, ff), BF16), sds((width, ff), BF16), sds((ff, width), BF16),
            sds((4, 4, 2, rows, width), BF16), sds((4, 4, 2, rows, width), BF16),
            sds((4, 4, 2, experts, rows), F32), sds((8, width + ff, width), BF16),
            sds((2, 2, rows, width), F32))
        vmem = pltpu.VMEM
        outs = pl.pallas_call(
            functools.partial(layer_kernel, side),
            out_shape=out_shape,
            in_specs=[any_spec] * 6,
            out_specs=[any_spec] * len(out_shape),
            scratch_shapes=[
                vmem((3, width + ff, width), BF16),
                vmem((4, rows, width), BF16), vmem((4, rows, width), BF16), vmem((4, experts, rows), F32),
                vmem((4, 2, rows, width), F32), vmem((2, 2, rows // 2, width), F32),
                vmem((width + ff, width), F32),
                vmem((2, 2, rows, width), BF16), vmem((2, 2, rows, width), BF16), vmem((2, 2, experts, rows), F32),
                vmem((2 * rows, ff), BF16), vmem((2 * rows, 2 * ff), BF16), vmem((2 * rows, width), BF16),
                vmem((width + ff, 2 * rows), BF16),
                pltpu.SemaphoreType.DMA((NUM_COPIES,)), pltpu.SemaphoreType.DMA((NUM_COPIES,)),
                pltpu.SemaphoreType.DMA((15,)),
            ],
            compiler_params=pltpu.CompilerParams(
                collective_id=0, has_side_effects=True, vmem_limit_bytes=66_900_000),
        )(x, dy, gate_t, w1[0], w3[0], w2[0])
        return outs[0], outs[1], outs[2][None], outs[3][None], outs[4][None]

    def layer_fn(tokens, expert_ids, gate_vals, w_gate, w_up, w_down, grad_out):
        return jax.shard_map(
            device_fn, mesh=mesh,
            in_specs=(tok_spec, tok_spec, tok_spec, w_spec, w_spec, w_spec, tok_spec),
            out_specs=(tok_spec, tok_spec, grad_spec, grad_spec, grad_spec), check_vma=False,
        )(tokens, expert_ids, gate_vals, w_gate, w_up, w_down, grad_out)

    return layer_fn
```

time: 1630 us -> 327 us (0.20)
  waiting for transfers between devices: 915 us -> 0 us
  matrix products: 355 us -> 0 us
  Pallas kernels: 0 us -> 311 us
  starting transfers between devices: 141 us -> 0 us
  local copies, waits for them, and re-layouts: 100 us -> 10.9 us
  other arithmetic: 84.1 us -> 1.46 us
    all_to_all x6 -> x0, waiting for transfers between devices: 915 us -> none  [the longest x1 277 us: device_fn(): hot_dx_back = lax.all_to_all(hot_dx[:, 0], 'ep', 0, 0)[owner_dev]]
    dot_general x18 -> x0, matrix products: 355 us -> none  [the longest x2 68 us: expert_backward(): jnp.einsum('secd,efd->secf', d_out_rows, down_w, preferred_element_type=j...]
    pallas_call x0 -> x1, Pallas kernels: none -> 311 us  [device_fn(): pl.pallas_call(functools.partial(layer_kernel, side), out_shape=out_shape...]
    all_to_all x6 -> x0, starting transfers between devices: 141 us -> none  [the longest x1 41.3 us: device_fn(): hot_dx_back = lax.all_to_all(hot_dx[:, 0], 'ep', 0, 0)[owner_dev]]
    gather x2 -> x0, local copies, waits for them, and re-layouts: 45 us -> none  [the longest x1 22.5 us: device_fn(): jnp.concatenate([cold_dx_back, hot_dx_back], axis=0)[buf_pos]]
    concatenate x2 -> x0, other arithmetic: 33 us -> none  [the longest x1 16.5 us: device_fn(): jnp.concatenate([cold_dx_back, hot_dx_back], axis=0)[buf_pos]]
    slice x4 -> x0, local copies, waits for them, and re-layouts: 25.1 us -> none  [the longest x1 10.5 us: device_fn(): cold_d = lax.all_to_all(send_d[:cold_rows].reshape(cold_shape), 'ep', 0, 0)]
    scatter x1 -> x0, other arithmetic: 23 us -> none  [scatter_rows(): jnp.zeros((buf_rows, row_vals.shape[-1]), row_vals.dtype).at[buf_pos]]
  transfers between devices with their start and end apart: 8 -> 0, of which waited for: 6 -> 0; matrix products, arithmetic and copies ran while one was open for 28% -> 0% of each run, Pallas kernels for 0% -> 0%
where the time goes in v1:
time: 327 us; the launch traced here: 324 us
  Pallas kernels  311 us (95%)
  local copies, waits for them, and re-layouts  10.9 us (3%)
    pallas_call x1, Pallas kernels, device_fn(): pl.pallas_call(functools.partial(layer_kernel, side), out_shape=out_shape...  311 us
    unnamed x5, local copies, waits for them, and re-layouts  10.9 us

profile of v1, /device:TPU:97, one launch (start us, length us, event | category | flops | bytes accessed | tf_op | source)
XLA Modules:
  0.0 324.0 jit_solution(16649409167279647737)
XLA Ops:
  0.6 1.5 select_reduce_fusion.g_ref
  2.1 311.0 %shard_map.110 = (bf16[384,1024]{1,0:T(8,128)(2,1)}, bf16[384,1024]{1,0:T(8,128)(2,1)}, bf16[1024,512]{1,0:T(8,128)(2,1)}, bf16[1024,512]{1,0:T(8,128)(2,1)}, bf...) custom-call(bf16[384,1024]{1,0:T(8,128)(2,1)} %x_ref.1, ...), custom_call_target="tpu_custom_call" | custom-call | tf_op jit(solution)/shard_map/pallas_call | solution.py:434
  313.1 2.1 copy.19
  315.1 2.1 copy.20
  317.2 2.3 copy.21
  319.4 2.3 copy.22
  321.7 2.3 copy.23

commit v2 on v1

--- a/solution.py
+++ b/solution.py
@@ -12,7 +12,7 @@
 F32 = jnp.float32
 BF16 = jnp.bfloat16
 NT = (((1,), (1,)), ((), ()))
-NUM_COPIES = 120
+NUM_COPIES = 122
 
 
 def dot(lhs, rhs):
@@ -84,8 +84,11 @@
                 reg((name + "p", j, i), own if (i, j) == (0, 0) else buf.at[j, i, 0], buf.at[j, i, 1], partner)
     reg(("r", "h+"), acc.at[3, :, pl.ds(0, half)], rs_half.at[0], xp)
     reg(("r", "h-"), acc.at[3, :, pl.ds(half, half)], rs_half.at[1], xm)
-    reg(("r", "+"), acc.at[1], rs_full.at[0], xp)
-    reg(("r", "-"), acc.at[2], rs_full.at[1], xm)
+    lo, hi = pl.ds(0, half), pl.ds(half, half)
+    reg(("r", "+a"), acc.at[1, :, hi], rs_full.at[0, :, hi], xp)
+    reg(("r", "-a"), acc.at[2, :, lo], rs_full.at[1, :, lo], xm)
+    reg(("r", "+b"), acc.at[1, :, lo], rs_full.at[0, :, lo], xp)
+    reg(("r", "-b"), acc.at[2, :, hi], rs_full.at[1, :, hi], xm)
 
     def start(*keys):
         for key in keys:
@@ -113,11 +116,12 @@
         pl.semaphore_signal(barrier, inc=1, device_id={"ep": target}, device_id_type=MESH)
     pl.semaphore_wait(barrier, 5)
 
+    start(("d", "y", "+"), ("d", "y", "-"))
     for name in ("g", "x", "d"):
         start((name, 0, "+"), (name, 0, "-"))
     for c in w_loads:
         c.wait()
-    start(("w", "+"), ("w", "-"), ("wp", 0), ("d", "y", "+"), ("d", "y", "-"))
+    start(("w", "+"), ("w", "-"), ("wp", 0))
     share("gxd", 0, 0)
     for c in t_loads:
         c.wait()
@@ -166,152 +170,50 @@
             dxp = dot_nt(dab_s[pl.ds(0, rows), :], wv[slot, pl.ds(n * nc, nc), :]).astype(BF16).astype(F32)
             acc[i, 1, :, cols] += jnp.where(routed, dxp, 0.0)
 
+    def run(copies_):
+        for c in copies_:
+            c.start()
+        for c in copies_:
+            c.wait()
+
+    def at_steps(s, pumps):
+        for k, pump in pumps.items():
+            pl.when(s == k)(pump)
+
+    def forward(name, key):
+        arrived((name, key, "+"), (name, key, "-"))
+        start((name, key, "2+"), (name, key, "2-"))
+
+    def partner_weights():
+        arrived(("wp", 0))
+        run([stage_w(1, 1)])
+
+    def row_neighbours():
+        for name in ("g", "x", "d"):
+            forward(name, 0)
+        arrived(("d", "y", "+"), ("d", "y", "-"))
+        start(("d", "y", "2+"), ("d", "y", "2-"))
+        for j in (1, 2):
+            start(("d", j, "+"), ("d", j, "-"))
+        for i in (1, 2):
+            share("gxd", 0, i)
+        run(stage_row(1, 9) + stage_row(2, 12))
+        for j in (1, 2):
+            share("d", j, 0)
+
+    def row_far():
+        for name in ("g", "x", "d"):
+            arrived((name, 0, "2+"), (name, 0, "2-"))
+        share("gxd", 0, 3)
+        run(stage_row(3, 9))
+
     def first_steps(s, carry):
         i, e = s // 2, lax.rem(s, 2)
-
-        @pl.when(s == 1)
-        def _():
-            arrived(("wp", 0))
-            c = stage_w(1, 1)
-            c.start()
-            c.wait()
-
-        @pl.when(s == 2)
-        def _():
-            for name in ("g", "x", "d"):
-                arrived((name, 0, "+"), (name, 0, "-"))
-                start((name, 0, "2+"), (name, 0, "2-"))
-            share("gxd", 0, 1)
-            share("gxd", 0, 2)
-            cs = stage_row(1, 9) + stage_row(2, 12)
-            for c in cs:
-                c.start()
-            for c in cs:
-                c.wait()
-
-        @pl.when(s == 6)
-        def _():
-            for name in ("g", "x", "d"):
-                arrived((name, 0, "2+"), (name, 0, "2-"))
-            share("gxd", 0, 3)
-            cs = stage_row(3, 9)
-            for c in cs:
-                c.start()
-            for c in cs:
-                c.wait()
-
+        at_steps(s, {1: partner_weights, 2: row_neighbours, 6: row_far})
         row_step(e, i, 0, e)
         return carry
 
     lax.fori_loop(0, 8, first_steps, 0)
-
-    arrived(("w", "+"), ("w", "-"))
-    start(("w", "2+"), ("w", "2-"), ("wp", 2), ("wp", 3))
-    stage_w(2, 2).start()
-
-    def middle_steps(s, carry):
-        k, i = s // 4, lax.rem(s, 4)
-        slot = 2 - lax.rem(k, 2)
-
-        @pl.when(i == 0)
-        def _():
-            stage_w(2, slot).wait()
-
-        @pl.when(i == 3)
-        def _():
-            @pl.when(k == 0)
-            def _():
-                stage_w(3, 1).start()
-
-            @pl.when(k == 1)
-            def _():
-                arrived(("wp", 2))
-                stage_w(4, 2).start()
-
-            @pl.when(k == 2)
-            def _():
-                arrived(("wp", 3))
-                stage_w(5, 1).start()
-
-            @pl.when(k == 3)
-            def _():
-                arrived(("w", "2+"), ("w", "2-"))
-                start(("wp", 6))
-                stage_w(6, 2).start()
-
-        @pl.when(s == 2)
-        def _():
-            arrived(("d", "y", "+"), ("d", "y", "-"))
-            start(("d", "y", "2+"), ("d", "y", "2-"))
-            for j in (1, 2):
-                start(("d", j, "+"), ("d", j, "-"))
-                share("d", j, 0)
-            for b in range(4):
-                for name in ("g", "x"):
-                    start((name, "y", b, "+"), (name, "y", b, "-"))
-
-        @pl.when(s == 9)
-        def _():
-            arrived(("d", "y", "2+"), ("d", "y", "2-"))
-            start(("d", 3, "+"), ("d", 3, "-"))
-            share("d", 3, 0)
-
-        for j, when in ((1, 11), (2, 14)):
-            @pl.when(s == when)
-            def _(j=j):
-                arrived(("d", j, "+"), ("d", j, "-"))
-                start(("d", j, "2+"), ("d", j, "2-"))
-                share("d", j, 1)
-                share("d", j, 2)
-
-        row_step(slot, i, 1 + 2 * lax.rem(k, 2), k // 2)
-        return carry
-
-    lax.fori_loop(0, 16, middle_steps, 0)
-    stage_w(6, 2).wait()
-
-    def pass_on_x(b):
-        for name in ("g", "x"):
-            arrived((name, "y", b, "+"), (name, "y", b, "-"))
-            start((name, "y", b, "2+"), (name, "y", b, "2-"))
-        share("gx", 1, b)
-        share("gx", 2, b)
-
-    def last_steps(s, carry):
-        i, e = 3 - s // 2, lax.rem(s, 2)
-
-        @pl.when(s == 1)
-        def _():
-            arrived(("wp", 6))
-            c = stage_w(7, 1)
-            c.start()
-            c.wait()
-
-        @pl.when(s == 2)
-        def _():
-            start(("r", "h+"), ("r", "h-"))
-            pass_on_x(0)
-
-        @pl.when(s == 4)
-        def _():
-            arrived(("d", 3, "+"), ("d", 3, "-"))
-            start(("d", 3, "2+"), ("d", 3, "2-"))
-            share("d", 3, 1)
-            share("d", 3, 2)
-            pass_on_x(1)
-
-        @pl.when(s == 6)
-        def _():
-            arrived(("r", "h+"), ("r", "h-"))
-            acc[1, :, pl.ds(0, half), :] += rs_half[0]
-            acc[2, :, pl.ds(half, half), :] += rs_half[1]
-            start(("r", "+"), ("r", "-"))
-            pass_on_x(2)
-
-        row_step(2 - e, i, 2, e)
-        return carry
-
-    lax.fori_loop(0, 8, last_steps, 0)
     for c in own_stores:
         c.wait()
 
@@ -319,10 +221,14 @@
         return [local(xg.at[j, i], xs.at[slot], 9 + slot), local(dg.at[j, i], ds.at[slot], 11 + slot),
                 local(gg.at[j, i], gs.at[slot], 13 + slot)]
 
-    def get_pair(j, i):
+    def get_pair(j, i, slot):
         arrived(("xp", j, i), ("gp", j, i), ("dp", j, i))
+        for c in stage_pair(j, i, slot):
+            c.start()
 
     def grad_step(slot):
+        for c in stage_pair(0, 0, slot):
+            c.wait()
         gate = jnp.concatenate([gate_columns(gs[slot, p, pl.ds(me, 1), :], nc) for p in range(2)], axis=0)
         x = xs[slot].reshape(2 * rows, width)
         routed = gate[:, :fc] > 0.0 if nc >= fc else jnp.concatenate([gate] * (fc // nc), axis=1) > 0.0
@@ -342,45 +248,127 @@
             dw[pl.ds(0, width), cols] += dot(xt_s[pl.ds(0, width), :], dab_s[:, cols])
             dw[pl.ds(width, ff), cols] += dot(xt_s[pl.ds(width, ff), :], do_s[:, cols])
 
-    get_pair(0, 0)
-    for c in stage_pair(0, 0, 0):
-        c.start()
+    get_pair(0, 0, 0)
+
+    def own_row_grads(q, carry):
+        at_steps(q, {i - 1: functools.partial(get_pair, 0, i, i % 2) for i in range(1, 4)})
+        grad_step(lax.rem(q, 2))
+        return carry
+
+    lax.fori_loop(0, 4, own_row_grads, 0)
+
+    forward("d", 1)
+    for i in (1, 2):
+        share("d", 1, i)
+    arrived(("w", "+"), ("w", "-"))
+    start(("w", "2+"), ("w", "2-"), ("wp", 2), ("wp", 3))
+    stage_w(2, 2).start()
+    for b in range(4):
+        for name in ("g", "x"):
+            start((name, "y", b, "+"), (name, "y", b, "-"))
+    forward("d", 2)
+    for i in (1, 2):
+        share("d", 2, i)
+
+    def cotangents_far():
+        arrived(("d", "y", "2+"), ("d", "y", "2-"))
+        start(("d", 3, "+"), ("d", 3, "-"))
+        share("d", 3, 0)
+
+    def cotangents_last():
+        forward("d", 3)
+        for i in (1, 2):
+            share("d", 3, i)
+
+    def next_weights(e):
+        if e == 6:
+            arrived(("w", "2+"), ("w", "2-"))
+            start(("wp", 6))
+        elif e > 3:
+            arrived(("wp", e - 2))
+        stage_w(e, 2 - e % 2).start()
+
+    def middle_steps(s, carry):
+        k, i = s // 4, lax.rem(s, 4)
+        slot = 2 - lax.rem(k, 2)
+
+        @pl.when(i == 0)
+        def _():
+            stage_w(2, slot).wait()
+
+        at_steps(s, {3: functools.partial(next_weights, 3), 4: cotangents_far, 7: functools.partial(next_weights, 4),
+                     11: functools.partial(next_weights, 5), 14: cotangents_last, 15: functools.partial(next_weights, 6)})
+        row_step(slot, i, 1 + 2 * lax.rem(k, 2), k // 2)
+        return carry
+
+    lax.fori_loop(0, 16, middle_steps, 0)
+    stage_w(6, 2).wait()
+
+    def far_weights():
+        arrived(("wp", 6))
+        run([stage_w(7, 1)])
+
+    def far_sums():
+        start(("r", "h+"), ("r", "h-"))
+        for j in (1, 2, 3):
+            arrived(("d", j, "2+"), ("d", j, "2-"))
+            share("d", j, 3)
+
+    def pass_on_x(b):
+        for name in ("g", "x"):
+            forward_y(name, b)
+        share("gx", 1, b)
+        share("gx", 2, b)
+
+    def forward_y(name, b):
+        arrived((name, "y", b, "+"), (name, "y", b, "-"))
+        start((name, "y", b, "2+"), (name, "y", b, "2-"))
+
+    def last_steps(s, carry):
+        i, e = 3 - s // 2, lax.rem(s, 2)
+        at_steps(s, {1: far_weights, 2: far_sums, 4: lambda: start(("r", "-a")), 6: lambda: start(("r", "+a"))})
+        row_step(2 - e, i, 2, e)
+        return carry
+
+    lax.fori_loop(0, 8, last_steps, 0)
+
+    def far_x(b):
+        for name in ("g", "x"):
+            arrived((name, "y", b, "2+"), (name, "y", b, "2-"))
+        share("gx", 3, b)
+
+    def pass_on_sums():
+        arrived(("r", "h+"), ("r", "h-"))
+        acc[1, :, lo, :] += rs_half[0]
+        acc[2, :, hi, :] += rs_half[1]
+        start(("r", "+b"), ("r", "-b"))
+
+    pairs = [(1 + q % 2, q // 2) for q in range(8)] + [(3, b) for b in range(4)]
+    pass_on_x(0)
+    get_pair(1, 0, 0)
+
+    def before_grad(q):
+        nj, ni = pairs[q + 1]
+        if nj == 2:
+            get_pair(nj, ni, (q + 1) % 2)
+
+    def after_grad(q):
+        nj, ni = pairs[q + 1]
+        if nj == 1:
+            pass_on_x(ni)
+        if nj == 3:
+            far_x(ni)
+        if nj != 2:
+            get_pair(nj, ni, (q + 1) % 2)
 
     def grad_steps(q, carry):
-        slot = lax.rem(q, 2)
-        nxt = q + 1
-        nj, ni = nxt // 4, lax.rem(nxt, 4)
-
-        @pl.when(q == 0)
-        def _():
-            pass_on_x(3)
-
-        for step in range(1, 16):
-            j, i = step // 4, step % 4
-
-            @pl.when(q == step - 1)
-            def _(j=j, i=i):
-                if j == 1 and i == 0:
-                    for jj in (1, 2, 3):
-                        arrived(("d", jj, "2+"), ("d", jj, "2-"))
-                        share("d", jj, 3)
-                if j == 2:
-                    for name in ("g", "x"):
-                        arrived((name, "y", i, "2+"), (name, "y", i, "2-"))
-                    share("gx", 3, i)
-                get_pair(j, i)
-
-        @pl.when(q < 15)
-        def _():
-            for c in stage_pair(nj, ni, 1 - slot):
-                c.start()
-
-        for c in stage_pair(0, 0, slot):
-            c.wait()
-        grad_step(slot)
+        at_steps(q, {4: pass_on_sums})
+        at_steps(q, {k: functools.partial(before_grad, k) for k in range(11)})
+        grad_step(lax.rem(q, 2))
+        at_steps(q, {k: functools.partial(after_grad, k) for k in range(11)})
         return carry
 
-    lax.fori_loop(0, 16, grad_steps, 0)
+    lax.fori_loop(0, 12, grad_steps, 0)
 
     outs = []
     wv[1] = dw[...].astype(BF16)
@@ -389,9 +377,10 @@
              local(wv.at[1, pl.ds(width, ff)], dw2_out, 2)]
     for c in outs:
         c.start()
-    arrived(("r", "+"), ("r", "-"))
-    copies[("r", "+")].wait_send()
-    copies[("r", "-")].wait_send()
+    sums = [("r", "+a"), ("r", "-a"), ("r", "+b"), ("r", "-b")]
+    arrived(*sums)
+    for key in sums:
+        copies[key].wait_send()
     fetch = [local(rs_full.at[0], acc.at[1], 3), local(rs_full.at[1], acc.at[2], 4)]
     for c in fetch:
         c.start()
@@ -403,10 +392,25 @@
         c.start()
         outs.append(c)
     for key, c in copies.items():
-        if key not in (("r", "+"), ("r", "-")):
+        if key not in sums:
             c.wait_send()
     for c in outs:
         c.wait()
+
+
+def copy_kernel(*refs):
+    n = (len(refs) - 1) // 3
+    srcs, dsts, bufs = refs[:n], refs[n:2 * n], refs[2 * n:3 * n]
+    sem = refs[3 * n]
+    ins = [pltpu.make_async_copy(s, b, sem.at[0, k]) for k, (s, b) in enumerate(zip(srcs, bufs))]
+    outs = [pltpu.make_async_copy(b, d, sem.at[1, k]) for k, (b, d) in enumerate(zip(bufs, dsts))]
+    for c in ins:
+        c.start()
+    for i, o in zip(ins, outs):
+        i.wait()
+        o.start()
+    for o in outs:
+        o.wait()
 
 
 def solution(mesh):
@@ -450,7 +454,15 @@
             compiler_params=pltpu.CompilerParams(
                 collective_id=0, has_side_effects=True, vmem_limit_bytes=66_900_000),
         )(x, dy, gate_t, w1[0], w3[0], w2[0])
-        return outs[0], outs[1], outs[2][None], outs[3][None], outs[4][None]
+        outs = outs[:5]
+        y, dx, dw1, dw3, dw2 = pl.pallas_call(
+            copy_kernel,
+            out_shape=[sds(o.shape, o.dtype) for o in outs],
+            in_specs=[any_spec] * 5,
+            out_specs=[any_spec] * 5,
+            scratch_shapes=[vmem(o.shape, o.dtype) for o in outs] + [pltpu.SemaphoreType.DMA((2, 5))],
+        )(*outs)
+        return y, dx, dw1[None], dw3[None], dw2[None]
 
     def layer_fn(tokens, expert_ids, gate_vals, w_gate, w_up, w_down, grad_out):
         return jax.shard_map(

time: 327 us -> 285 us (0.87)
  Pallas kernels: 311 us -> 282 us
  local copies, waits for them, and re-layouts: 10.9 us -> 0 us
    pallas_call x1, Pallas kernels: 311 us -> 278 us  [device_fn(): pl.pallas_call(functools.partial(layer_kernel, side), out_shape=out_shape...]
    unnamed x5 -> x0, local copies, waits for them, and re-layouts: 10.9 us -> none
    pallas_call x0 -> x1, Pallas kernels: none -> 4.06 us  [device_fn(): pl.pallas_call(copy_kernel, out_shape=[sds(o.shape, o.dtype) for o in out...]
where the time goes in v2:
time: 285 us; the launch traced here: 284 us
  Pallas kernels  282 us (99%)
    pallas_call x1, Pallas kernels, device_fn(): pl.pallas_call(functools.partial(layer_kernel, side), out_shape=out_shape...  278 us

profile of v2, /device:TPU:97, one launch (start us, length us, event | category | flops | bytes accessed | tf_op | source)
XLA Modules:
  0.0 284.2 jit_solution(9529353521268769976)
XLA Ops:
  0.6 1.5 select_reduce_fusion.g_ref
  2.1 277.9 %shard_map.110 = (bf16[384,1024]{1,0:T(8,128)(2,1)}, bf16[384,1024]{1,0:T(8,128)(2,1)}, bf16[1024,512]{1,0:T(8,128)(2,1)}, bf16[1024,512]{1,0:T(8,128)(2,1)}, bf...) custom-call(bf16[384,1024]{1,0:T(8,128)(2,1)} %x_ref.1, ...), custom_call_target="tpu_custom_call" | custom-call | tf_op jit(solution)/shard_map/pallas_call | solution.py:438
  280.0 4.1 %shard_map.111 = (bf16[384,1024]{1,0:T(8,128)(2,1)}, bf16[384,1024]{1,0:T(8,128)(2,1)}, bf16[1024,512]{1,0:T(8,128)(2,1)}, bf16[1024,512]{1,0:T(8,128)(2,1)}, bf16[512,1024]{1,0:T(8,128)(2,1)}) custom-call(bf16[384,1024]{1,0:T(8,128)(2,1)} %get-tuple-element.15.refs_0_, bf16[384,1024]{1,0:T(8,128)(2,1)} %get-tuple-element.16.refs_1_, ...), custom_call_target="tpu_custom_call" | custom-call | tf_op jit(solution)/shard_map/pallas_call | solution.py:458

commit v3 on v2

--- a/solution.py
+++ b/solution.py
@@ -12,7 +12,7 @@
 F32 = jnp.float32
 BF16 = jnp.bfloat16
 NT = (((1,), (1,)), ((), ()))
-NUM_COPIES = 122
+NUM_COPIES = 101
 
 
 def dot(lhs, rhs):
@@ -29,8 +29,8 @@
 
 
 def layer_kernel(side, x_ref, dy_ref, g_ref, w1_ref, w3_ref, w2_ref,
-                 y_out, dx_out, dw1_out, dw3_out, dw2_out, xg, dg, gg, wg, rs_full,
-                 wv, xrow, dyrow, grow, acc, rs_half, dw, xs, ds, gs, u_s, dab_s, do_s, xt_s,
+                 y_out, dx_out, dw1_out, dw3_out, dw2_out, xg, dg, gg, gy, wg,
+                 wv, xrow, dyrow, grow, acc, rs_half, rs_full, dw, xs, ds, gs, u_s, dab_s, do_s, xt_s,
                  send_sem, recv_sem, loc_sem):
     rows, width = x_ref.shape
     ff = w1_ref.shape[1]
@@ -69,19 +69,24 @@
     reg(("wp", 2), wg.at[2], wg.at[4], partner)
     reg(("wp", 3), wg.at[3], wg.at[5], partner)
     reg(("wp", 6), wg.at[6], wg.at[7], partner)
-    for name, own, buf, n in (("x", x_ref, xg, rows), ("g", g_ref, gg, g_ref.shape[0])):
-        reg_ring((name, 0), xp, xm, own, lambda s, buf=buf: buf.at[0, s, 0], n)
-        for i in range(4):
-            src = own if i == 0 else buf.at[0, i, 0]
-            reg_ring((name, "y", i), yp, ym, src, lambda s, buf=buf, i=i: buf.at[s, i, 0], n)
+    column = pl.ds(pl.multiple_of(px * (2 * side), 2 * side), 2 * side)
+    reg_ring(("x", 0), xp, xm, x_ref, lambda s: xg.at[0, s, 0], rows)
+    reg_ring(("g", 0), xp, xm, g_ref, lambda s: gg.at[s, 0], g_ref.shape[0])
+    for i in range(4):
+        src = x_ref if i == 0 else xg.at[0, i, 0]
+        reg_ring(("x", "y", i), yp, ym, src, lambda s, i=i: xg.at[s, i, 0], rows)
+    reg_ring(("g", "y"), yp, ym, gg.at[:, 0, column], lambda s: gy.at[s, 0], 4)
     reg_ring(("d", "y"), yp, ym, dy_ref, lambda s: dg.at[s, 0, 0], rows)
     for j in range(4):
         src = dy_ref if j == 0 else dg.at[j, 0, 0]
         reg_ring(("d", j), xp, xm, src, lambda s, j=j: dg.at[j, s, 0], rows)
-    for name, own, buf in (("x", x_ref, xg), ("g", g_ref, gg), ("d", dy_ref, dg)):
-        for j in range(4):
-            for i in range(4):
-                reg((name + "p", j, i), own if (i, j) == (0, 0) else buf.at[j, i, 0], buf.at[j, i, 1], partner)
+    for j in range(4):
+        for i in range(4):
+            reg(("xp", j, i), x_ref if (i, j) == (0, 0) else xg.at[j, i, 0], xg.at[j, i, 1], partner)
+            reg(("dp", j, i), dy_ref if (i, j) == (0, 0) else dg.at[j, i, 0], dg.at[j, i, 1], partner)
+        reg(("gp", 0, j), g_ref if j == 0 else gg.at[j, 0], gg.at[j, 1], partner)
+        if j:
+            reg(("gyp", j), gy.at[j, 0], gy.at[j, 1], partner)
     reg(("r", "h+"), acc.at[3, :, pl.ds(0, half)], rs_half.at[0], xp)
     reg(("r", "h-"), acc.at[3, :, pl.ds(half, half)], rs_half.at[1], xm)
     lo, hi = pl.ds(0, half), pl.ds(half, half)
@@ -126,7 +131,7 @@
     for c in t_loads:
         c.wait()
     own_stores = [local(xrow.at[0], xg.at[0, 0, 0], 3), local(dyrow.at[0], dg.at[0, 0, 0], 4),
-                  local(grow.at[0], gg.at[0, 0, 0], 5)]
+                  local(grow.at[0], gg.at[0, 0], 5)]
     for c in own_stores:
         c.start()
     for b in range(4):
@@ -136,7 +141,7 @@
 
     def stage_row(i, k):
         return [local(xg.at[0, i, 0], xrow.at[i], k), local(dg.at[0, i, 0], dyrow.at[i], k + 1),
-                local(gg.at[0, i, 0], grow.at[i], k + 2)]
+                local(gg.at[i, 0], grow.at[i], k + 2)]
 
     def stage_w(e, slot):
         return local(wg.at[e], wv.at[slot], 6 + slot)
@@ -152,7 +157,7 @@
         return hidden, da, db
 
     def row_step(slot, i, jrel, plane):
-        expert = dev(py + jrel, px, lax.rem(core + plane, 2))
+        expert = (px * side + lax.rem(py + jrel, side)) * 2 + lax.rem(core + plane, 2)
         gate = gate_columns(grow[i, pl.ds(expert, 1), :], nc)
         routed = gate > 0.0
         for n in range(4):
@@ -218,18 +223,21 @@
         c.wait()
 
     def stage_pair(j, i, slot):
+        gates = gg.at[i, :, column] if j == 0 else gy.at[j, :, i]
         return [local(xg.at[j, i], xs.at[slot], 9 + slot), local(dg.at[j, i], ds.at[slot], 11 + slot),
-                local(gg.at[j, i], gs.at[slot], 13 + slot)]
+                local(gates, gs.at[slot], 13 + slot)]
 
     def get_pair(j, i, slot):
-        arrived(("xp", j, i), ("gp", j, i), ("dp", j, i))
+        arrived(("xp", j, i), ("dp", j, i))
+        if j == 0:
+            arrived(("gp", 0, i))
         for c in stage_pair(j, i, slot):
             c.start()
 
     def grad_step(slot):
         for c in stage_pair(0, 0, slot):
             c.wait()
-        gate = jnp.concatenate([gate_columns(gs[slot, p, pl.ds(me, 1), :], nc) for p in range(2)], axis=0)
+        gate = jnp.concatenate([gate_columns(gs[slot, p, pl.ds(2 * py + core, 1), :], nc) for p in range(2)], axis=0)
         x = xs[slot].reshape(2 * rows, width)
         routed = gate[:, :fc] > 0.0 if nc >= fc else jnp.concatenate([gate] * (fc // nc), axis=1) > 0.0
         for n in range(4):
@@ -263,9 +271,9 @@
     arrived(("w", "+"), ("w", "-"))
     start(("w", "2+"), ("w", "2-"), ("wp", 2), ("wp", 3))
     stage_w(2, 2).start()
+    start(("g", "y", "+"), ("g", "y", "-"))
     for b in range(4):
-        for name in ("g", "x"):
-            start((name, "y", b, "+"), (name, "y", b, "-"))
+        start(("x", "y", b, "+"), ("x", "y", b, "-"))
     forward("d", 2)
     for i in (1, 2):
         share("d", 2, i)
@@ -289,19 +297,19 @@
         stage_w(e, 2 - e % 2).start()
 
     def middle_steps(s, carry):
-        k, i = s // 4, lax.rem(s, 4)
+        k, i = s // 3, 3 - lax.rem(s, 3)
         slot = 2 - lax.rem(k, 2)
 
-        @pl.when(i == 0)
+        @pl.when(i == 3)
         def _():
             stage_w(2, slot).wait()
 
-        at_steps(s, {3: functools.partial(next_weights, 3), 4: cotangents_far, 7: functools.partial(next_weights, 4),
-                     11: functools.partial(next_weights, 5), 14: cotangents_last, 15: functools.partial(next_weights, 6)})
+        at_steps(s, {2: functools.partial(next_weights, 3), 3: cotangents_far, 5: functools.partial(next_weights, 4),
+                     8: functools.partial(next_weights, 5), 10: cotangents_last, 11: functools.partial(next_weights, 6)})
         row_step(slot, i, 1 + 2 * lax.rem(k, 2), k // 2)
         return carry
 
-    lax.fori_loop(0, 16, middle_steps, 0)
+    lax.fori_loop(0, 12, middle_steps, 0)
     stage_w(6, 2).wait()
 
     def far_weights():
@@ -314,28 +322,37 @@
             arrived(("d", j, "2+"), ("d", j, "2-"))
             share("d", j, 3)
 
+        forward("g", "y")
+        for j in (1, 2):
+            start(("gyp", j))
+
     def pass_on_x(b):
-        for name in ("g", "x"):
-            forward_y(name, b)
-        share("gx", 1, b)
-        share("gx", 2, b)
-
-    def forward_y(name, b):
-        arrived((name, "y", b, "+"), (name, "y", b, "-"))
-        start((name, "y", b, "2+"), (name, "y", b, "2-"))
+        arrived(("x", "y", b, "+"), ("x", "y", b, "-"))
+        start(("x", "y", b, "2+"), ("x", "y", b, "2-"))
+        share("x", 1, b)
+        share("x", 2, b)
 
     def last_steps(s, carry):
         i, e = 3 - s // 2, lax.rem(s, 2)
-        at_steps(s, {1: far_weights, 2: far_sums, 4: lambda: start(("r", "-a")), 6: lambda: start(("r", "+a"))})
+        at_steps(s, {1: far_weights, 2: far_sums, 4: lambda: start(("r", "-a")), 6: lambda: start(("r", "+a")),
+                     7: lambda: stage_w(2, 2).start()})
         row_step(2 - e, i, 2, e)
         return carry
 
     lax.fori_loop(0, 8, last_steps, 0)
 
+    def own_steps(k, carry):
+        slot = 2 - lax.rem(k, 2)
+        stage_w(2, slot).wait()
+        at_steps(k, {e - 3: (lambda e=e: stage_w(e, 2 - e % 2).start()) for e in (3, 4, 5)})
+        row_step(slot, 0, 1 + 2 * lax.rem(k, 2), k // 2)
+        return carry
+
+    lax.fori_loop(0, 4, own_steps, 0)
+
     def far_x(b):
-        for name in ("g", "x"):
-            arrived((name, "y", b, "2+"), (name, "y", b, "2-"))
-        share("gx", 3, b)
+        arrived(("x", "y", b, "2+"), ("x", "y", b, "2-"))
+        share("x", 3, b)
 
     def pass_on_sums():
         arrived(("r", "h+"), ("r", "h-"))
@@ -345,6 +362,9 @@
 
     pairs = [(1 + q % 2, q // 2) for q in range(8)] + [(3, b) for b in range(4)]
     pass_on_x(0)
+    arrived(("g", "y", "2+"), ("g", "y", "2-"))
+    start(("gyp", 3))
+    arrived(("gyp", 1), ("gyp", 2), ("gyp", 3))
     get_pair(1, 0, 0)
 
     def before_grad(q):
@@ -362,7 +382,7 @@
             get_pair(nj, ni, (q + 1) % 2)
 
     def grad_steps(q, carry):
-        at_steps(q, {4: pass_on_sums})
+        at_steps(q, {2: pass_on_sums})
         at_steps(q, {k: functools.partial(before_grad, k) for k in range(11)})
         grad_step(lax.rem(q, 2))
         at_steps(q, {k: functools.partial(after_grad, k) for k in range(11)})
@@ -370,30 +390,20 @@
 
     lax.fori_loop(0, 12, grad_steps, 0)
 
-    outs = []
     wv[1] = dw[...].astype(BF16)
-    outs += [local(wv.at[1, pl.ds(0, width), pl.ds(0, ff)], dw1_out, 0),
-             local(wv.at[1, pl.ds(0, width), pl.ds(ff, ff)], dw3_out, 1),
-             local(wv.at[1, pl.ds(width, ff)], dw2_out, 2)]
+    outs = [local(wv.at[1, pl.ds(0, width), pl.ds(0, ff)], dw1_out, 0),
+            local(wv.at[1, pl.ds(0, width), pl.ds(ff, ff)], dw3_out, 1),
+            local(wv.at[1, pl.ds(width, ff)], dw2_out, 2)]
     for c in outs:
         c.start()
-    sums = [("r", "+a"), ("r", "-a"), ("r", "+b"), ("r", "-b")]
-    arrived(*sums)
-    for key in sums:
-        copies[key].wait_send()
-    fetch = [local(rs_full.at[0], acc.at[1], 3), local(rs_full.at[1], acc.at[2], 4)]
-    for c in fetch:
-        c.start()
-    for c in fetch:
-        c.wait()
+    arrived(("r", "+a"), ("r", "-a"), ("r", "+b"), ("r", "-b"))
     for v, (buf, out) in enumerate(((xrow, y_out), (dyrow, dx_out))):
-        buf[1] = (acc[0, v] + acc[1, v] + acc[2, v]).astype(BF16)
+        buf[1] = (acc[0, v] + rs_full[0, v] + rs_full[1, v]).astype(BF16)
         c = local(buf.at[1], out, 3 + v)
         c.start()
         outs.append(c)
     for key, c in copies.items():
-        if key not in sums:
-            c.wait_send()
+        c.wait_send()
     for c in outs:
         c.wait()
 
@@ -424,7 +434,8 @@
         rows, width = x.shape
         ff = w1.shape[2]
         experts = group_size * w1.shape[0]
-        onehot = ids[None, :, :] == jnp.arange(experts, dtype=ids.dtype)[:, None, None]
+        order = jnp.arange(experts, dtype=ids.dtype).reshape(side, side, 2).swapaxes(0, 1).reshape(experts)
+        onehot = ids[None, :, :] == order[:, None, None]
         gate_t = jnp.sum(jnp.where(onehot, gates[None, :, :], 0.0), axis=2)
         any_spec = pl.BlockSpec(memory_space=pl.ANY)
         sds = jax.ShapeDtypeStruct
@@ -432,8 +443,7 @@
             sds((rows, width), BF16), sds((rows, width), BF16),
             sds((width, ff), BF16), sds((width, ff), BF16), sds((ff, width), BF16),
             sds((4, 4, 2, rows, width), BF16), sds((4, 4, 2, rows, width), BF16),
-            sds((4, 4, 2, experts, rows), F32), sds((8, width + ff, width), BF16),
-            sds((2, 2, rows, width), F32))
+            sds((4, 2, experts, rows), F32), sds((4, 2, 4, 2 * side, rows), F32), sds((8, width + ff, width), BF16))
         vmem = pltpu.VMEM
         outs = pl.pallas_call(
             functools.partial(layer_kernel, side),
@@ -444,8 +454,9 @@
                 vmem((3, width + ff, width), BF16),
                 vmem((4, rows, width), BF16), vmem((4, rows, width), BF16), vmem((4, experts, rows), F32),
                 vmem((4, 2, rows, width), F32), vmem((2, 2, rows // 2, width), F32),
+                vmem((2, 2, rows, width), F32),
                 vmem((width + ff, width), F32),
-                vmem((2, 2, rows, width), BF16), vmem((2, 2, rows, width), BF16), vmem((2, 2, experts, rows), F32),
+                vmem((2, 2, rows, width), BF16), vmem((2, 2, rows, width), BF16), vmem((2, 2, 2 * side, rows), F32),
                 vmem((2 * rows, ff), BF16), vmem((2 * rows, 2 * ff), BF16), vmem((2 * rows, width), BF16),
                 vmem((width + ff, 2 * rows), BF16),
                 pltpu.SemaphoreType.DMA((NUM_COPIES,)), pltpu.SemaphoreType.DMA((NUM_COPIES,)),

time: 285 us -> 315 us (1.11)
  Pallas kernels: 282 us -> 312 us
    pallas_call x1, Pallas kernels: 278 us -> 308 us  [device_fn(): pl.pallas_call(functools.partial(layer_kernel, side), out_shape=out_shape...]
where the time goes in v3:
time: 315 us
  Pallas kernels  312 us (99%)
    pallas_call x1, Pallas kernels, device_fn(): pl.pallas_call(functools.partial(layer_kernel, side), out_shape=out_shape...  308 us

profile of v3, /device:TPU:97, one launch (start us, length us, event | category | flops | bytes accessed | tf_op | source)
XLA Modules:
  0.0 314.7 jit_solution(14716544008682712941)
XLA Ops:
  0.6 0.1 reshape.61
  0.7 1.5 select_reduce_fusion.g_ref
  2.3 308.2 %shard_map.110 = (bf16[384,1024]{1,0:T(8,128)(2,1)}, bf16[384,1024]{1,0:T(8,128)(2,1)}, bf16[1024,512]{1,0:T(8,128)(2,1)}, bf16[1024,512]{1,0:T(8,128)(2,1)}, bf...) custom-call(bf16[384,1024]{1,0:T(8,128)(2,1)} %x_ref.1, ...), custom_call_target="tpu_custom_call" | custom-call | tf_op jit(solution)/shard_map/pallas_call | solution.py:448
  310.5 4.1 %shard_map.111 = (bf16[384,1024]{1,0:T(8,128)(2,1)}, bf16[384,1024]{1,0:T(8,128)(2,1)}, bf16[1024,512]{1,0:T(8,128)(2,1)}, bf16[1024,512]{1,0:T(8,128)(2,1)}, bf16[512,1024]{1,0:T(8,128)(2,1)}) custom-call(bf16[384,1024]{1,0:T(8,128)(2,1)} %get-tuple-element.15.refs_0_, bf16[384,1024]{1,0:T(8,128)(2,1)} %get-tuple-element.16.refs_1_, ...), custom_call_target="tpu_custom_call" | custom-call | tf_op jit(solution)/shard_map/pallas_call | solution.py:469
  (1 shorter events, 0.0 us)

commit v4 on v3

--- a/solution.py
+++ b/solution.py
@@ -221,6 +221,7 @@
     lax.fori_loop(0, 8, first_steps, 0)
     for c in own_stores:
         c.wait()
+    start(("g", "y", "+"), ("g", "y", "-"))
 
     def stage_pair(j, i, slot):
         gates = gg.at[i, :, column] if j == 0 else gy.at[j, :, i]
@@ -271,9 +272,6 @@
     arrived(("w", "+"), ("w", "-"))
     start(("w", "2+"), ("w", "2-"), ("wp", 2), ("wp", 3))
     stage_w(2, 2).start()
-    start(("g", "y", "+"), ("g", "y", "-"))
-    for b in range(4):
-        start(("x", "y", b, "+"), ("x", "y", b, "-"))
     forward("d", 2)
     for i in (1, 2):
         share("d", 2, i)
@@ -282,6 +280,11 @@
         arrived(("d", "y", "2+"), ("d", "y", "2-"))
         start(("d", 3, "+"), ("d", 3, "-"))
         share("d", 3, 0)
+        forward("g", "y")
+        for j in (1, 2):
+            start(("gyp", j))
+        for b in range(4):
+            start(("x", "y", b, "+"), ("x", "y", b, "-"))
 
     def cotangents_last():
         forward("d", 3)
@@ -322,9 +325,8 @@
             arrived(("d", j, "2+"), ("d", j, "2-"))
             share("d", j, 3)
 
-        forward("g", "y")
-        for j in (1, 2):
-            start(("gyp", j))
+        arrived(("g", "y", "2+"), ("g", "y", "2-"))
+        start(("gyp", 3))
 
     def pass_on_x(b):
         arrived(("x", "y", b, "+"), ("x", "y", b, "-"))
@@ -362,8 +364,6 @@
 
     pairs = [(1 + q % 2, q // 2) for q in range(8)] + [(3, b) for b in range(4)]
     pass_on_x(0)
-    arrived(("g", "y", "2+"), ("g", "y", "2-"))
-    start(("gyp", 3))
     arrived(("gyp", 1), ("gyp", 2), ("gyp", 3))
     get_pair(1, 0, 0)
 

time: 315 us -> 289 us (0.917)
  Pallas kernels: 312 us -> 286 us
    pallas_call x1, Pallas kernels: 308 us -> 282 us  [device_fn(): pl.pallas_call(functools.partial(layer_kernel, side), out_shape=out_shape...]
where the time goes in v4:
time: 289 us
  Pallas kernels  286 us (99%)
    pallas_call x1, Pallas kernels, device_fn(): pl.pallas_call(functools.partial(layer_kernel, side), out_shape=out_shape...  282 us

profile of v4, /device:TPU:97, one launch (start us, length us, event | category | flops | bytes accessed | tf_op | source)
XLA Modules:
  0.0 288.5 jit_solution(2764489883350844770)
XLA Ops:
  0.6 0.1 reshape.61
  0.7 1.5 select_reduce_fusion.g_ref
  2.3 282.0 %shard_map.110 = (bf16[384,1024]{1,0:T(8,128)(2,1)}, bf16[384,1024]{1,0:T(8,128)(2,1)}, bf16[1024,512]{1,0:T(8,128)(2,1)}, bf16[1024,512]{1,0:T(8,128)(2,1)}, bf...) custom-call(bf16[384,1024]{1,0:T(8,128)(2,1)} %x_ref.1, ...), custom_call_target="tpu_custom_call" | custom-call | tf_op jit(solution)/shard_map/pallas_call | solution.py:448
  284.3 4.1 %shard_map.111 = (bf16[384,1024]{1,0:T(8,128)(2,1)}, bf16[384,1024]{1,0:T(8,128)(2,1)}, bf16[1024,512]{1,0:T(8,128)(2,1)}, bf16[1024,512]{1,0:T(8,128)(2,1)}, bf16[512,1024]{1,0:T(8,128)(2,1)}) custom-call(bf16[384,1024]{1,0:T(8,128)(2,1)} %get-tuple-element.15.refs_0_, bf16[384,1024]{1,0:T(8,128)(2,1)} %get-tuple-element.16.refs_1_, ...), custom_call_target="tpu_custom_call" | custom-call | tf_op jit(solution)/shard_map/pallas_call | solution.py:469
  (1 shorter events, 0.0 us)

commit v5 on v4

--- a/solution.py
+++ b/solution.py
@@ -300,7 +300,8 @@
         stage_w(e, 2 - e % 2).start()
 
     def middle_steps(s, carry):
-        k, i = s // 3, 3 - lax.rem(s, 3)
+        tail = s // 12
+        k, i = (s - tail) // 3, 3 - lax.rem(s, 3) - 3 * tail
         slot = 2 - lax.rem(k, 2)
 
         @pl.when(i == 3)
@@ -308,11 +309,12 @@
             stage_w(2, slot).wait()
 
         at_steps(s, {2: functools.partial(next_weights, 3), 3: cotangents_far, 5: functools.partial(next_weights, 4),
-                     8: functools.partial(next_weights, 5), 10: cotangents_last, 11: functools.partial(next_weights, 6)})
+                     8: functools.partial(next_weights, 5), 11: cotangents_last})
         row_step(slot, i, 1 + 2 * lax.rem(k, 2), k // 2)
         return carry
 
-    lax.fori_loop(0, 12, middle_steps, 0)
+    lax.fori_loop(0, 13, middle_steps, 0)
+    next_weights(6)
     stage_w(6, 2).wait()
 
     def far_weights():
@@ -335,22 +337,30 @@
         share("x", 2, b)
 
     def last_steps(s, carry):
-        i, e = 3 - s // 2, lax.rem(s, 2)
-        at_steps(s, {1: far_weights, 2: far_sums, 4: lambda: start(("r", "-a")), 6: lambda: start(("r", "+a")),
-                     7: lambda: stage_w(2, 2).start()})
+        late = s // 4
+        i = (1 - late) * (3 - lax.rem(s, 2)) + late * (3 - s // 2)
+        e = (1 - late) * (s // 2) + late * lax.rem(s, 2)
+        at_steps(s, {2: far_weights, 3: far_sums, 4: lambda: start(("r", "-a")), 6: lambda: start(("r", "+a")),
+                     7: near_x})
         row_step(2 - e, i, 2, e)
         return carry
 
+    def near_x():
+        stage_w(2, 2).start()
+        pass_on_x(0)
+
     lax.fori_loop(0, 8, last_steps, 0)
+    arrived(("gyp", 1), ("gyp", 2), ("gyp", 3))
+    get_pair(1, 0, 0)
 
     def own_steps(k, carry):
         slot = 2 - lax.rem(k, 2)
         stage_w(2, slot).wait()
-        at_steps(k, {e - 3: (lambda e=e: stage_w(e, 2 - e % 2).start()) for e in (3, 4, 5)})
+        at_steps(k, {0: lambda: stage_w(3, 1).start(), 1: lambda: stage_w(4, 2).start(), 2: lambda: pass_on_x(1)})
         row_step(slot, 0, 1 + 2 * lax.rem(k, 2), k // 2)
         return carry
 
-    lax.fori_loop(0, 4, own_steps, 0)
+    lax.fori_loop(0, 3, own_steps, 0)
 
     def far_x(b):
         arrived(("x", "y", b, "2+"), ("x", "y", b, "2-"))
@@ -363,22 +373,19 @@
         start(("r", "+b"), ("r", "-b"))
 
     pairs = [(1 + q % 2, q // 2) for q in range(8)] + [(3, b) for b in range(4)]
-    pass_on_x(0)
-    arrived(("gyp", 1), ("gyp", 2), ("gyp", 3))
-    get_pair(1, 0, 0)
+    before = {3: lambda: pass_on_x(2), 5: lambda: pass_on_x(3), 7: lambda: far_x(0), 8: lambda: far_x(1),
+              9: lambda: far_x(2), 10: lambda: far_x(3)}
 
     def before_grad(q):
+        if q in before:
+            before[q]()
         nj, ni = pairs[q + 1]
-        if nj == 2:
+        if nj == 2 or (nj, ni) == (1, 1):
             get_pair(nj, ni, (q + 1) % 2)
 
     def after_grad(q):
         nj, ni = pairs[q + 1]
-        if nj == 1:
-            pass_on_x(ni)
-        if nj == 3:
-            far_x(ni)
-        if nj != 2:
+        if not (nj == 2 or (nj, ni) == (1, 1)):
             get_pair(nj, ni, (q + 1) % 2)
 
     def grad_steps(q, carry):

time: 289 us -> 266 us (0.920)
  Pallas kernels: 286 us -> 263 us
    pallas_call x1, Pallas kernels: 282 us -> 259 us  [device_fn(): pl.pallas_call(functools.partial(layer_kernel, side), out_shape=out_shape...]
where the time goes in v5:
time: 266 us; the launch traced here: 265 us
  Pallas kernels  263 us (99%)
    pallas_call x1, Pallas kernels, device_fn(): pl.pallas_call(functools.partial(layer_kernel, side), out_shape=out_shape...  259 us

profile of v5, /device:TPU:97, one launch (start us, length us, event | category | flops | bytes accessed | tf_op | source)
XLA Modules:
  0.0 265.3 jit_solution(4467318798074317383)
XLA Ops:
  0.6 0.1 reshape.61
  0.7 1.5 select_reduce_fusion.g_ref
  2.3 258.8 %shard_map.110 = (bf16[384,1024]{1,0:T(8,128)(2,1)}, bf16[384,1024]{1,0:T(8,128)(2,1)}, bf16[1024,512]{1,0:T(8,128)(2,1)}, bf16[1024,512]{1,0:T(8,128)(2,1)}, bf...) custom-call(bf16[384,1024]{1,0:T(8,128)(2,1)} %x_ref.1, ...), custom_call_target="tpu_custom_call" | custom-call | tf_op jit(solution)/shard_map/pallas_call | solution.py:455
  261.1 4.1 %shard_map.111 = (bf16[384,1024]{1,0:T(8,128)(2,1)}, bf16[384,1024]{1,0:T(8,128)(2,1)}, bf16[1024,512]{1,0:T(8,128)(2,1)}, bf16[1024,512]{1,0:T(8,128)(2,1)}, bf16[512,1024]{1,0:T(8,128)(2,1)}) custom-call(bf16[384,1024]{1,0:T(8,128)(2,1)} %get-tuple-element.15.refs_0_, bf16[384,1024]{1,0:T(8,128)(2,1)} %get-tuple-element.16.refs_1_, ...), custom_call_target="tpu_custom_call" | custom-call | tf_op jit(solution)/shard_map/pallas_call | solution.py:476
  (1 shorter events, 0.0 us)

commit v6 on v5

--- a/solution.py
+++ b/solution.py
@@ -68,7 +68,7 @@
     reg(("wp", 0), wv.at[0], wg.at[1], partner)
     reg(("wp", 2), wg.at[2], wg.at[4], partner)
     reg(("wp", 3), wg.at[3], wg.at[5], partner)
-    reg(("wp", 6), wg.at[6], wg.at[7], partner)
+    reg(("wp", 6), wg.at[6], wv.at[3], partner)
     column = pl.ds(pl.multiple_of(px * (2 * side), 2 * side), 2 * side)
     reg_ring(("x", 0), xp, xm, x_ref, lambda s: xg.at[0, s, 0], rows)
     reg_ring(("g", 0), xp, xm, g_ref, lambda s: gg.at[s, 0], g_ref.shape[0])
@@ -235,7 +235,7 @@
         for c in stage_pair(j, i, slot):
             c.start()
 
-    def grad_step(slot):
+    def grad_step(slot, between):
         for c in stage_pair(0, 0, slot):
             c.wait()
         gate = jnp.concatenate([gate_columns(gs[slot, p, pl.ds(2 * py + core, 1), :], nc) for p in range(2)], axis=0)
@@ -250,6 +250,7 @@
             u_s[:, pl.ds(h * fc, fc)] = jnp.where(routed, hidden, 0.0).astype(BF16)
             dab_s[:, pl.ds(h * fc, fc)] = jnp.where(routed, da, 0.0).astype(BF16)
             dab_s[:, pl.ds(ff + h * fc, fc)] = jnp.where(routed, db, 0.0).astype(BF16)
+        between()
         xt_s[pl.ds(0, width), :] = jnp.transpose(x)
         xt_s[pl.ds(width, ff), :] = jnp.transpose(u_s[...])
         for n in range(4):
@@ -261,7 +262,7 @@
 
     def own_row_grads(q, carry):
         at_steps(q, {i - 1: functools.partial(get_pair, 0, i, i % 2) for i in range(1, 4)})
-        grad_step(lax.rem(q, 2))
+        grad_step(lax.rem(q, 2), lambda: None)
         return carry
 
     lax.fori_loop(0, 4, own_row_grads, 0)
@@ -319,7 +320,6 @@
 
     def far_weights():
         arrived(("wp", 6))
-        run([stage_w(7, 1)])
 
     def far_sums():
         start(("r", "h+"), ("r", "h-"))
@@ -342,7 +342,7 @@
         e = (1 - late) * (s // 2) + late * lax.rem(s, 2)
         at_steps(s, {2: far_weights, 3: far_sums, 4: lambda: start(("r", "-a")), 6: lambda: start(("r", "+a")),
                      7: near_x})
-        row_step(2 - e, i, 2, e)
+        row_step(2 + e, i, 2, e)
         return carry
 
     def near_x():
@@ -383,7 +383,7 @@
         if nj == 2 or (nj, ni) == (1, 1):
             get_pair(nj, ni, (q + 1) % 2)
 
-    def after_grad(q):
+    def mid_grad(q):
         nj, ni = pairs[q + 1]
         if not (nj == 2 or (nj, ni) == (1, 1)):
             get_pair(nj, ni, (q + 1) % 2)
@@ -391,8 +391,7 @@
     def grad_steps(q, carry):
         at_steps(q, {2: pass_on_sums})
         at_steps(q, {k: functools.partial(before_grad, k) for k in range(11)})
-        grad_step(lax.rem(q, 2))
-        at_steps(q, {k: functools.partial(after_grad, k) for k in range(11)})
+        grad_step(lax.rem(q, 2), lambda: at_steps(q, {k: functools.partial(mid_grad, k) for k in range(11)}))
         return carry
 
     lax.fori_loop(0, 12, grad_steps, 0)
@@ -450,7 +449,7 @@
             sds((rows, width), BF16), sds((rows, width), BF16),
             sds((width, ff), BF16), sds((width, ff), BF16), sds((ff, width), BF16),
             sds((4, 4, 2, rows, width), BF16), sds((4, 4, 2, rows, width), BF16),
-            sds((4, 2, experts, rows), F32), sds((4, 2, 4, 2 * side, rows), F32), sds((8, width + ff, width), BF16))
+            sds((4, 2, experts, rows), F32), sds((4, 2, 4, 2 * side, rows), F32), sds((7, width + ff, width), BF16))
         vmem = pltpu.VMEM
         outs = pl.pallas_call(
             functools.partial(layer_kernel, side),
@@ -458,7 +457,7 @@
             in_specs=[any_spec] * 6,
             out_specs=[any_spec] * len(out_shape),
             scratch_shapes=[
-                vmem((3, width + ff, width), BF16),
+                vmem((4, width + ff, width), BF16),
                 vmem((4, rows, width), BF16), vmem((4, rows, width), BF16), vmem((4, experts, rows), F32),
                 vmem((4, 2, rows, width), F32), vmem((2, 2, rows // 2, width), F32),
                 vmem((2, 2, rows, width), F32),

time: 266 us -> 260 us (0.977)
  Pallas kernels: 263 us -> 257 us
    pallas_call x1, Pallas kernels: 259 us -> 253 us  [device_fn(): pl.pallas_call(functools.partial(layer_kernel, side), out_shape=out_shape...]
where the time goes in v6:
time: 260 us
  Pallas kernels  257 us (99%)
    pallas_call x1, Pallas kernels, device_fn(): pl.pallas_call(functools.partial(layer_kernel, side), out_shape=out_shape...  253 us

profile of v6, /device:TPU:97, one launch (start us, length us, event | category | flops | bytes accessed | tf_op | source)
XLA Modules:
  0.0 259.9 jit_solution(10761909229659478209)
XLA Ops:
  0.6 0.1 reshape.61
  0.7 1.5 select_reduce_fusion.g_ref
  2.3 253.4 %shard_map.110 = (bf16[384,1024]{1,0:T(8,128)(2,1)}, bf16[384,1024]{1,0:T(8,128)(2,1)}, bf16[1024,512]{1,0:T(8,128)(2,1)}, bf16[1024,512]{1,0:T(8,128)(2,1)}, bf...) custom-call(bf16[384,1024]{1,0:T(8,128)(2,1)} %x_ref.1, ...), custom_call_target="tpu_custom_call" | custom-call | tf_op jit(solution)/shard_map/pallas_call | solution.py:454
  255.7 4.1 %shard_map.111 = (bf16[384,1024]{1,0:T(8,128)(2,1)}, bf16[384,1024]{1,0:T(8,128)(2,1)}, bf16[1024,512]{1,0:T(8,128)(2,1)}, bf16[1024,512]{1,0:T(8,128)(2,1)}, bf16[512,1024]{1,0:T(8,128)(2,1)}) custom-call(bf16[384,1024]{1,0:T(8,128)(2,1)} %get-tuple-element.15.refs_0_, bf16[384,1024]{1,0:T(8,128)(2,1)} %get-tuple-element.16.refs_1_, ...), custom_call_target="tpu_custom_call" | custom-call | tf_op jit(solution)/shard_map/pallas_call | solution.py:475
  (1 shorter events, 0.0 us)
